TPU v7x, 128 devices: a whole 4x4x4 slice. The times are simulated.
128 devices in a mesh: dp: 16 (over y, x), seq: 8 (over z, core).
Axes of the slice: x: 4, y: 4, z: 4, core: 2. Of those that a mesh axis runs over, the one named last changes fastest.
Arguments:
- hidden_in: bfloat16 [16, 1024, 2048], P('dp', 'seq'), may hold values from -6 to 6
- cotangent: bfloat16 [16, 1024, 2048], P('dp', 'seq'), may hold values from -6 to 6
- norm_gain: float32 [2048], P('dp'), may hold values from 0.1 to 1.9
- route_weights: float32 [16, 1024, 10], P('dp', 'seq'), may hold values from 0.1 to 1
- expert_ids: int32 [16, 1024, 10], P('dp', 'seq'), may hold values from 0 to 255, all different within a row; in each aligned block of 128 rows (0 to 127, 128 to 255, ..., all dimensions but the last counted through in order) at most 6 rows name the same one
- expert_gate: bfloat16 [256, 2048, 512], P(('dp', 'seq')), may hold values from -0.125 to 0.125
- expert_up: bfloat16 [256, 2048, 512], P(('dp', 'seq')), may hold values from -0.125 to 0.125
- expert_down: bfloat16 [256, 512, 2048], P(('dp', 'seq')), may hold values from -0.25 to 0.25
Outputs:
- grad_hidden: bfloat16 [16, 1024, 2048], P('dp', 'seq')
- grad_gain: float32 [2048], P('dp')
- grad_gate: bfloat16 [256, 2048, 512], P(('dp', 'seq'))
- grad_up: bfloat16 [256, 2048, 512], P(('dp', 'seq'))
- grad_down: bfloat16 [256, 512, 2048], P(('dp', 'seq'))
Inputs may be any that keep to these rules, and one draw needn't show every extreme that they name: `expert_ids`: each token names 10 different experts. Among the rows of one device no expert is named by more than 6 of them, and in some device one expert is named by exactly 6.
All inputs are finite; a program needn't handle non-finite values.
Results may differ from a plain program's by a relative error of at most 0.0072.
Values may be sent and summed in bfloat16 or wider, within the bound.
A program may use at most 192 MiB of HBM per device.

v0:
```python
import jax
import jax.numpy as jnp
from jax import lax
from jax.sharding import PartitionSpec as P

TOP = 10


EPSILON = 1e-06


def joined_along(parts, dim):
    shape = list(parts.shape[1:])
    shape[dim] *= parts.shape[0]
    return jnp.moveaxis(parts, 0, dim).reshape(shape)


def from_everyone(x, axis):
    peers = lax.axis_size(axis)
    return lax.all_to_all(jnp.broadcast_to(x[None], (peers, *x.shape)), axis, 0, 0, tiled=True)


def collect(x, axis, dim):
    return joined_along(from_everyone(x, axis), dim)


def sent_together(arrays, axis, split_dim, concat_dim, along):
    both = jnp.concatenate(arrays, axis=along)
    out, at, done = (
        lax.all_to_all(both, axis, split_axis=split_dim, concat_axis=concat_dim, tiled=True),
        0,
        [],
    )
    for a in arrays:
        done.append(lax.slice_in_dim(out, at, at + a.shape[along], axis=along))
        at += a.shape[along]
    return tuple(done)


def split_up(x, dim, peers):
    before, after = (x.shape[:dim], x.shape[dim + 1 :])
    return jnp.moveaxis(x.reshape(*before, peers, -1, *after), dim, 0)


def summed_on_arrival(x, axis, dim):
    peers = lax.axis_size(axis)
    parts = lax.all_to_all(split_up(x, dim, peers), axis, 0, 0, tiled=True)
    return jnp.sum(parts, axis=0)


def over_copies(x, axis):
    everything = from_everyone(x, axis)
    return jnp.sum(everything, axis=0)


def shards(
    hidden_in, cotangent, norm_gain, route_weights, expert_ids, expert_gate, expert_up, expert_down
):
    tokens_here = hidden_in.shape[1]
    model_width = hidden_in.shape[2]
    local_experts = expert_gate.shape[0]
    dp_count = lax.axis_size("dp")
    seq_count = lax.axis_size("seq")
    devices = dp_count * seq_count
    expert_count = local_experts * devices
    capacity = max(2, tokens_here * TOP * 6 // (5 * expert_count))
    assignments = tokens_here * TOP
    gain_full = collect(norm_gain, "dp", 0)
    inputs = hidden_in[0].astype(jnp.float32)
    inverse_root = lax.rsqrt(jnp.mean(inputs * inputs, axis=1, keepdims=True) + EPSILON)
    scaled = inputs * inverse_root
    normed = (scaled * gain_full[None, :]).astype(jnp.bfloat16)
    upstream = cotangent[0]
    weighted = (route_weights[0][:, :, None] * upstream[:, None, :].astype(jnp.float32)).astype(
        jnp.bfloat16
    )
    weighted = weighted.reshape(assignments, model_width)
    flat_experts = expert_ids[0].reshape(assignments)
    onehot = (flat_experts[:, None] == jnp.arange(expert_count, dtype=jnp.int32)[None, :]).astype(
        jnp.bfloat16
    )
    position = jnp.arange(assignments, dtype=jnp.int32)
    earlier = (position[:, None] > position[None, :]).astype(jnp.bfloat16)
    before = jnp.dot(earlier, onehot, preferred_element_type=jnp.float32)
    earlier_count = jnp.sum(before * onehot.astype(jnp.float32), axis=1).astype(jnp.int32)
    slot_index = flat_experts * capacity + earlier_count
    slot_entry = jnp.zeros((expert_count * capacity,), jnp.int32).at[slot_index].set(position + 1)
    occupied = slot_entry > 0
    source = jnp.maximum(slot_entry - 1, 0)
    zero_value = jnp.zeros((), jnp.bfloat16)
    flat_shape = (devices, local_experts * capacity, model_width)
    send_rows = jnp.where(occupied[:, None], normed[source // TOP], zero_value).reshape(flat_shape)
    send_grads = jnp.where(occupied[:, None], weighted[source], zero_value).reshape(flat_shape)
    arrived_rows, arrived_grads = sent_together((send_rows, send_grads), ("dp", "seq"), 0, 0, 1)
    four_shape = (devices, local_experts, capacity, model_width)
    rows_in = arrived_rows.reshape(four_shape)
    rows_grad = arrived_grads.reshape(four_shape)
    pre_gate = jnp.einsum(
        "nicd,idf->nicf", rows_in, expert_gate, preferred_element_type=jnp.float32
    )
    pre_up = jnp.einsum("nicd,idf->nicf", rows_in, expert_up, preferred_element_type=jnp.float32)
    sigmoid_gate = jax.nn.sigmoid(pre_gate)
    silu_gate = pre_gate * sigmoid_gate
    activation = (silu_gate * pre_up).astype(jnp.bfloat16)
    grad_act = jnp.einsum(
        "nicd,ifd->nicf", rows_grad, expert_down, preferred_element_type=jnp.float32
    )
    gate_back = (grad_act * pre_up * sigmoid_gate * (1.0 + pre_gate * (1.0 - sigmoid_gate))).astype(
        jnp.bfloat16
    )
    up_back = (grad_act * silu_gate).astype(jnp.bfloat16)
    grad_down = jnp.einsum(
        "nicf,nicd->ifd", activation, rows_grad, preferred_element_type=jnp.float32
    ).astype(jnp.bfloat16)
    grad_gate = jnp.einsum(
        "nicd,nicf->idf", rows_in, gate_back, preferred_element_type=jnp.float32
    ).astype(jnp.bfloat16)
    grad_up = jnp.einsum(
        "nicd,nicf->idf", rows_in, up_back, preferred_element_type=jnp.float32
    ).astype(jnp.bfloat16)
    returned = (
        jnp.einsum("nicf,idf->nicd", gate_back, expert_gate, preferred_element_type=jnp.float32)
        + jnp.einsum("nicf,idf->nicd", up_back, expert_up, preferred_element_type=jnp.float32)
    ).astype(jnp.bfloat16)
    back_rows = lax.all_to_all(
        returned.reshape(flat_shape), ("dp", "seq"), split_axis=0, concat_axis=0, tiled=True
    )
    back_flat = back_rows.reshape(expert_count * capacity, model_width)
    summed = jnp.sum(
        back_flat[slot_index].astype(jnp.float32).reshape(tokens_here, TOP, model_width), axis=1
    )
    local_gain = jnp.sum(summed * scaled, axis=0)
    partial_share = summed_on_arrival(local_gain, "dp", 0)
    grad_gain = over_copies(partial_share, "seq")
    gained = summed * gain_full[None, :]
    centered = jnp.mean(gained * scaled, axis=1, keepdims=True)
    grad_hidden = (
        upstream.astype(jnp.float32) + inverse_root * (gained - scaled * centered)
    ).astype(jnp.bfloat16)
    return (grad_hidden.reshape(hidden_in.shape), grad_gain, grad_gate, grad_up, grad_down)


def solution(mesh):
    return jax.shard_map(
        shards,
        mesh=mesh,
        in_specs=(
            P("dp", "seq", None),
            P("dp", "seq", None),
            P("dp"),
            P("dp", "seq", None),
            P("dp", "seq", None),
            P(("dp", "seq"), None, None),
            P(("dp", "seq"), None, None),
            P(("dp", "seq"), None, None),
        ),
        out_specs=(
            P("dp", "seq", None),
            P("dp"),
            P(("dp", "seq"), None, None),
            P(("dp", "seq"), None, None),
            P(("dp", "seq"), None, None),
        ),
        check_vma=False,
    )
```

profile of v0, /device:TPU:1, one launch (start us, length us, event | category | flops | bytes accessed | tf_op | source)
XLA Modules:
  0.0 508.7 jit_solution(3446099808075103148)
XLA Ops:
  0.6 1.3 broadcast_in_dim.47
  1.9 7.6 %all-to-all-start = ((f32[16,1,128]{2,1,0:T(1,128)}), f32[16,1,128]{2,1,0:T(1,128)S(1)}, u32[]{:S(2)}, u32[]{:S(2)}) async-start(f32[16,1,128]{2,1,0:T(1,128)} %broadcast_in_dim.47), calls=%async_computation | async-start | bytes 16384 | tf_op jit(solution)/shard_map/all_to_all | solution.py:20
  9.5 0.7 broadcast_multiply_fusion
  10.2 0.8 copy.38
  11.0 0.1 copy.37
  11.1 0.1 mul.127
  11.2 0.1 eq.15
  11.4 0.0 copy-start
  11.4 0.0 copy-start.12
  11.4 0.0 copy-start.5
  11.4 1.1 fusion.27
  12.5 5.2 %scatter_custom_fusion = s32[1536]{0:T(1024)S(1)} fusion(s32[1280]{0:T(1024)S(1)} %fusion.38, s32[1280]{0:T(1024)S(1)} %iota_add_fusion, s32[]{:T(128)} %constant.15.clone.1), kind=kCustom, calls=%fused_computation.74 | custom fusion | bytes 6148 | tf_op jit(solution)/shard_map/scatter | solution.py:87
  17.8 0.2 fusion.32
  18.0 0.0 copy-start.13
  18.0 0.1 copy.39
  18.1 0.1 mul.134
  18.3 0.1 convert_bitcast_fusion.1
  18.4 7.9 %mul.136 = f32[128,10,2048]{2,1,0:T(8,128)} broadcast(f32[128,2048]{1,0:T(8,128)S(1)} %convert_bitcast_fusion.1), dimensions={0,2} | broadcast | bytes 11534336 | tf_op jit(solution)/shard_map/mul | solution.py:74
  26.3 13.9 %mul.137 = f32[1280,2048]{1,0:T(8,128)} reshape(f32[128,10,2048]{2,1,0:T(8,128)} %mul.136) | data formatting | bytes 20971520 | tf_op jit(solution)/shard_map/mul | solution.py:74
  40.3 6.9 %multiply_convert_fusion = bf16[1280,2048]{1,0:T(8,128)(2,1)} fusion(f32[1280,2048]{1,0:T(8,128)} %mul.137, f32[1280]{0:T(1024)S(1)} %mul.134), kind=kLoop, calls=%fused_computation.6 | loop fusion | flops 5242880 | bytes 15733760 | tf_op jit(solution)/shard_map/convert_element_type | solution.py:74
  47.2 0.1 broadcast_in_dim.26
  47.3 15.9 %gather_fusion.1 = bf16[1536,2048]{1,0:T(8,128)(2,1)} fusion(bf16[1280,2048]{1,0:T(8,128)(2,1)} %multiply_convert_fusion, s32[2048]{0:T(1024)S(1)} %pad_clamp_fusion.1), kind=kCustom, calls=%fused_computation.1 | custom fusion | bytes 12589056 | tf_op jit(solution)/shard_map/gather | solution.py:93
  63.2 10.6 %gather.16 = bf16[128,12,2048]{2,1,0:T(8,128)(2,1)} reshape(bf16[1536,2048]{1,0:T(8,128)(2,1)} %gather_fusion.1) | data formatting | bytes 12582912 | tf_op jit(solution)/shard_map/gather | solution.py:93
  73.8 0.2 fusion.29
  74.0 7.1 %gather_fusion = bf16[1536,2048]{1,0:T(8,128)(2,1)} fusion(bf16[128,2048]{1,0:T(8,128)(2,1)S(1)} %fusion.29, s32[2048]{0:T(1024)S(1)} %pad_clamp_fusion.2), kind=kCustom, calls=%fused_computation | custom fusion | bytes 12589056 | tf_op jit(solution)/shard_map/gather | solution.py:92
  81.0 10.6 %gather.14 = bf16[128,12,2048]{2,1,0:T(8,128)(2,1)} reshape(bf16[1536,2048]{1,0:T(8,128)(2,1)} %gather_fusion) | data formatting | bytes 12582912 | tf_op jit(solution)/shard_map/gather | solution.py:92
  91.6 6.6 %broadcast_select_fusion.1 = (bf16[128,12,2048]{2,1,0:T(8,128)(2,1)S(1)}, bf16[128,12,2048]{2,1,0:T(8,128)(2,1)S(1)}) fusion(bf16[128,12,2048]{2,1,0:T(8,128)(2,1)} %gather.14, pred[128,12]{1,0:T(8,128)(4,1)S(1)} %broadcast_in_dim.26, bf16[128,12,2048]{2,1,0:T(8,128)(2,1)} %gather.16), kind=kLoop, calls=%fused_computation.11 | loop fusion | flops 6291456 | bytes 25167360 | tf_op jit(solution)/shard_map/jit(_where)/select_n | solution.py:92
  98.2 6.1 %pad_maximum_fusion = bf16[128,24,2048]{2,1,0:T(8,128)(2,1)S(1)} fusion(bf16[128,12,2048]{2,1,0:T(8,128)(2,1)S(1)} %get-tuple-element.12, bf16[128,12,2048]{2,1,0:T(8,128)(2,1)S(1)} %get-tuple-element.11), kind=kLoop, calls=%fused_computation.4 | loop fusion | flops 25165824 | bytes 25165824 | tf_op jit(solution)/shard_map/concatenate | solution.py:28
  104.4 154.7 %all_to_all.31 = bf16[128,24,2048]{2,1,0:T(8,128)(2,1)S(1)} all-to-all(bf16[128,24,2048]{2,1,0:T(8,128)(2,1)S(1)} %pad_maximum_fusion), channel_id=1, replica_groups=mesh['dp'=16,'seq'=8] {'dp','seq'}, dimensions={0} | all-to-all | bytes 25165824 | tf_op jit(solution)/shard_map/all_to_all | solution.py:30
  259.1 6.0 %fusion.42 = (bf16[128,12,2048]{2,1,0:T(8,128)(2,1)}, bf16[128,12,2048]{2,1,0:T(8,128)(2,1)S(1)}) fusion(bf16[128,24,2048]{2,1,0:T(8,128)(2,1)S(1)} %all_to_all.31), kind=kLoop, calls=%fused_computation.80 | loop fusion | bytes 25165824 | tf_op jit(solution)/shard_map/slice | solution.py:35
  265.1 9.5 %copy.40 = bf16[128,12,2048]{2,0,1:T(8,128)(2,1)} copy(bf16[128,12,2048]{2,1,0:T(8,128)(2,1)} %get-tuple-element.7) | data formatting | bytes 12582912 | tf_op jit(solution)/shard_map/slice | solution.py:35
  274.5 6.1 %copy.41 = bf16[128,12,2048]{2,0,1:T(8,128)(2,1)} copy(bf16[128,12,2048]{2,1,0:T(8,128)(2,1)S(1)} %get-tuple-element.8) | data formatting | bytes 12582912 | tf_op jit(solution)/shard_map/slice | solution.py:35
  280.6 8.0 %fusion.3 = f32[2,128,6,512]{3,1,2,0:T(8,128)} fusion(bf16[128,2,6,2048]{3,0,2,1:T(8,128)(2,1)} %bitcast.127, bf16[2,2048,512]{2,1,0:T(8,128)(2,1)S(1)} %copy-done.3), kind=kOutput, calls=%fused_computation.16 | convolution fusion | flops 3221225472 | bytes 13631488 | tf_op jit(solution)/shard_map/nicd,idf->nicf/dot_general | solution.py:98
  288.6 5.1 %fusion.8 = f32[2,128,6,512]{3,1,2,0:T(8,128)} fusion(bf16[128,2,6,2048]{3,0,2,1:T(8,128)(2,1)S(1)} %bitcast.129, bf16[2,2048,512]{2,1,0:T(8,128)(2,1)S(1)} %copy-done.4), kind=kOutput, calls=%fused_computation.21 | convolution fusion | flops 3221225472 | bytes 13631488 | tf_op jit(solution)/shard_map/nicd,idf->nicf/dot_general | solution.py:101
  293.7 8.2 %fusion.18 = (bf16[128,2,6,512]{3,0,2,1:T(8,128)(2,1)S(1)}, bf16[128,2,6,512]{3,0,2,1:T(8,128)(2,1)S(1)}) fusion(f32[2,128,6,512]{3,1,2,0:T(8,128)} %fusion.3, f32[2,128,6,512]{3,1,2,0:T(8,128)} %fusion.8, bf16[128,2,6,2048]{3,0,2,1:T(8,128)(2,1)S(1)} %bitcast.123, bf16[2,512,2048]{2,1,0:T(8,128)(2,1)} %param.15), kind=kOutput, calls=%fused_computation.37 | convolution fusion | flops 3231449088 | bytes 19922944 | tf_op jit(solution)/shard_map/nicd,ifd->nicf/dot_general | solution.py:105
  301.9 0.0 copy-start.7
  301.9 0.0 copy-start.9
  301.9 6.4 %fusion.1 = f32[2,128,6,2048]{3,1,2,0:T(8,128)} fusion(bf16[128,2,6,512]{3,0,2,1:T(8,128)(2,1)S(1)} %get-tuple-element.10, bf16[2,2048,512]{2,1,0:T(8,128)(2,1)S(1)} %copy-done.3), kind=kOutput, calls=%fused_computation.14 | convolution fusion | flops 3221225472 | bytes 18350080 | tf_op jit(solution)/shard_map/nicf,idf->nicd/dot_general | solution.py:122
  308.3 7.7 %add_convert_fusion = bf16[2,128,6,2048]{3,1,2,0:T(8,128)(2,1)S(1)} fusion(f32[2,128,6,2048]{3,1,2,0:T(8,128)} %fusion.1, bf16[128,2,6,512]{3,0,2,1:T(8,128)(2,1)S(1)} %get-tuple-element.9, bf16[2,2048,512]{2,1,0:T(8,128)(2,1)} %param.14), kind=kOutput, calls=%fused_computation.5 | convolution fusion | flops 3227516928 | bytes 24641536 | tf_op jit(solution)/shard_map/nicf,idf->nicd/dot_general | solution.py:123
  316.0 6.9 %copy.42 = bf16[128,12,2048]{2,1,0:T(8,128)(2,1)} copy(bf16[128,12,2048]{2,0,1:T(8,128)(2,1)S(1)} %bitcast.120) | data formatting | bytes 12582912 | tf_op jit(solution)/shard_map/reshape | solution.py:126
  322.9 10.4 %all-to-all-start.2 = ((bf16[128,12,2048]{2,1,0:T(8,128)(2,1)}), bf16[128,12,2048]{2,1,0:T(8,128)(2,1)}, u32[]{:S(2)}, u32[]{:S(2)}) async-start(bf16[128,12,2048]{2,1,0:T(8,128)(2,1)} %copy.42), calls=%async_computation.2 | async-start | bytes 16777216 | tf_op jit(solution)/shard_map/all_to_all | solution.py:125
  333.3 0.0 slice-start.5
  333.3 0.0 copy-start.8
  333.3 0.0 slice-start.2
  333.3 8.9 %bitcast_convert_fusion.1 = bf16[2,2048,512]{2,1,0:T(8,128)(2,1)} fusion(bf16[128,2,6,2048]{3,0,2,1:T(8,128)(2,1)} %bitcast.128, bf16[128,2,6,512]{3,0,2,1:T(8,128)(2,1)} %copy-done.9), kind=kOutput, calls=%fused_computation.8 | convolution fusion | flops 3223322624 | bytes 12058624 | tf_op jit(solution)/shard_map/nicd,nicf->idf/dot_general | solution.py:118
  342.2 5.1 bitcast_convert_fusion.2
  347.3 8.3 %bitcast_convert_fusion = bf16[2,512,2048]{2,1,0:T(8,128)(2,1)} fusion(bf16[128,2,6,2048]{3,0,2,1:T(8,128)(2,1)S(1)} %bitcast.126, f32[2,128,6,512]{3,1,2,0:T(8,128)} %fusion.8, f32[2,128,6,512]{3,1,2,0:T(8,128)} %fusion.3), kind=kOutput, calls=%fused_computation.7 | convolution fusion | flops 3228041216 | bytes 16777216 | tf_op jit(solution)/shard_map/nicf,nicd->ifd/dot_general | solution.py:112
  355.6 78.8 %all-to-all-done.2 = bf16[128,12,2048]{2,1,0:T(8,128)(2,1)} async-done(((bf16[128,12,2048]{2,1,0:T(8,128)(2,1)}), bf16[128,12,2048]{2,1,0:T(8,128)(2,1)}, u32[]{:S(2)}, u32[]{:S(2)}) %all-to-all-start.2) | async-done | bytes 6291488 | tf_op jit(solution)/shard_map/all_to_all | solution.py:125
  434.4 10.7 %reshape.175 = bf16[1536,2048]{1,0:T(8,128)(2,1)} reshape(bf16[128,12,2048]{2,1,0:T(8,128)(2,1)} %all-to-all-done.2) | data formatting | bytes 12582912 | tf_op jit(solution)/shard_map/reshape | solution.py:128
  445.1 14.4 %gather_fusion.2 = bf16[1280,2048]{1,0:T(8,128)(2,1)} fusion(bf16[1536,2048]{1,0:T(8,128)(2,1)} %reshape.175, s32[2048]{0:T(1024)S(1)} %pad_clamp_fusion), kind=kCustom, calls=%fused_computation.2 | custom fusion | bytes 10490880 | tf_op jit(solution)/shard_map/gather | solution.py:130
  459.5 10.5 %reshape.178 = f32[128,10,2048]{2,1,0:T(8,128)} reshape(bf16[1280,2048]{1,0:T(8,128)(2,1)} %gather_fusion.2) | data formatting | bytes 15728640 | tf_op jit(solution)/shard_map/convert_element_type | solution.py:130
  470.0 0.0 copy-start.1
  470.0 0.0 copy-start.11
  470.1 0.0 copy-start.14
  470.1 0.0 copy-start.6
  470.1 9.9 %reduce_sum.67 = f32[128,2048]{1,0:T(8,128)S(1)} reduce(f32[128,10,2048]{2,1,0:T(8,128)} %reshape.178, f32[]{:T(128)} %constant.12.clone.1), dimensions={1}, to_apply=%region_3.4 | reduce | flops 2359296 | bytes 11534340 | tf_op jit(solution)/shard_map/reduce_sum | solution.py:129
  480.0 0.9 fusion.31
  480.9 9.6 %all-to-all-start.3 = ((f32[16,1,128]{2,1,0:T(1,128)}), f32[16,1,128]{2,1,0:T(1,128)S(1)}, u32[]{:S(2)}, u32[]{:S(2)}) async-start(f32[16,1,128]{2,1,0:T(1,128)} %bitcast.18), calls=%async_computation.3 | async-start | bytes 16384 | tf_op jit(solution)/shard_map/all_to_all | solution.py:47
  490.5 6.3 %all-to-all-done.3 = f32[16,1,128]{2,1,0:T(1,128)S(1)} async-done(((f32[16,1,128]{2,1,0:T(1,128)}), f32[16,1,128]{2,1,0:T(1,128)S(1)}, u32[]{:S(2)}, u32[]{:S(2)}) %all-to-all-start.3) | async-done | bytes 8224 | tf_op jit(solution)/shard_map/all_to_all | solution.py:47
  496.8 0.6 broadcast_in_dim.51
  497.4 5.6 %all-to-all-start.4 = ((f32[8,1,128]{2,1,0:T(1,128)}), f32[8,1,128]{2,1,0:T(1,128)S(1)}, u32[]{:S(2)}, u32[]{:S(2)}) async-start(f32[8,1,128]{2,1,0:T(1,128)} %broadcast_in_dim.51), calls=%async_computation.4 | async-start | bytes 8192 | tf_op jit(solution)/shard_map/all_to_all | solution.py:20
  503.1 1.2 fusion.28
  504.3 3.4 all-to-all-done.4
  507.7 0.5 reduce_sum.72
  (44 shorter events, 0.2 us)
Async XLA Ops:
  1.9 71.9 %all-to-all-start = ((f32[16,1,128]{2,1,0:T(1,128)}), f32[16,1,128]{2,1,0:T(1,128)S(1)}, u32[]{:S(2)}, u32[]{:S(2)}) async-start(f32[16,1,128]{2,1,0:T(1,128)} %broadcast_in_dim.47), calls=%async_computation | async-start | bytes 16384 | tf_op jit(solution)/shard_map/all_to_all | solution.py:20
  11.4 6.4 %copy-start = (bf16[1,128,2048]{2,1,0:T(8,128)(2,1)S(1)}, bf16[1,128,2048]{2,1,0:T(8,128)(2,1)}, u32[]{:S(2)}) copy-start(bf16[1,128,2048]{2,1,0:T(8,128)(2,1)} %param.8) | copy-start | bytes 1572868
  11.4 6.6 %copy-start.12 = (f32[1,128,10]{1,0,2:T(1,128)S(1)}, f32[1,128,10]{1,0,2:T(1,128)}, u32[]{:S(2)}) copy-start(f32[1,128,10]{1,0,2:T(1,128)} %param.11) | copy-start | bytes 15364
  11.4 6.9 %copy-start.5 = (bf16[1,128,2048]{2,1,0:T(8,128)(2,1)S(1)}, bf16[1,128,2048]{2,1,0:T(8,128)(2,1)}, u32[]{:S(2)}) copy-start(bf16[1,128,2048]{2,1,0:T(8,128)(2,1)} %param.9) | copy-start | bytes 1572868
  18.0 55.8 %copy-start.13 = (f32[128]{0:T(128)}, f32[128]{0:T(128)S(1)}, u32[]{:S(2)}) copy-start(f32[128]{0:T(128)S(1)} %add_rsqrt_fusion) | copy-start | bytes 1540
  73.8 7.3 %copy-start.10 = (f32[16,1,128]{2,1,0:T(1,128)}, f32[16,1,128]{2,1,0:T(1,128)S(1)}, u32[]{:S(2)}) copy-start(f32[16,1,128]{2,1,0:T(1,128)S(1)} %all-to-all-done) | copy-start | bytes 24580
  274.5 6.1 %copy-start.3 = (bf16[2,2048,512]{2,1,0:T(8,128)(2,1)S(1)}, bf16[2,2048,512]{2,1,0:T(8,128)(2,1)}, u32[]{:S(2)}) copy-start(bf16[2,2048,512]{2,1,0:T(8,128)(2,1)} %param.13) | copy-start | bytes 12582916
  280.6 8.0 %copy-start.2 = (bf16[128,12,2048]{2,0,1:T(8,128)(2,1)S(1)}, bf16[128,12,2048]{2,0,1:T(8,128)(2,1)}, u32[]{:S(2)}) copy-start(bf16[128,12,2048]{2,0,1:T(8,128)(2,1)} %copy.41) | copy-start | bytes 18874372
  280.6 8.0 %copy-start.4 = (bf16[2,2048,512]{2,1,0:T(8,128)(2,1)S(1)}, bf16[2,2048,512]{2,1,0:T(8,128)(2,1)}, u32[]{:S(2)}) copy-start(bf16[2,2048,512]{2,1,0:T(8,128)(2,1)} %param.14) | copy-start | bytes 12582916
  280.6 13.1 %slice-start = ((s8[6291456]{0:T(1024)(128)(4,1)}), s8[4194304]{0:T(1024)(128)(4,1)S(1)}, s32[]{:S(2)}) async-start(s8[6291456]{0:T(1024)(128)(4,1)} %bitcast.121), calls=%async_computation.5 | async-start | bytes 8388608
  288.6 5.1 %slice-start.1 = ((s8[6291456]{0:T(1024)(128)(4,1)}), s8[2097152]{0:T(1024)(128)(4,1)S(1)}, s32[]{:S(2)}) async-start(s8[6291456]{0:T(1024)(128)(4,1)} %bitcast.121), calls=%async_computation.6 | async-start | bytes 4194304
  301.9 6.4 %copy-start.7 = (bf16[128,2,6,512]{3,0,2,1:T(8,128)(2,1)}, bf16[128,2,6,512]{3,0,2,1:T(8,128)(2,1)S(1)}, u32[]{:S(2)}) copy-start(bf16[128,2,6,512]{3,0,2,1:T(8,128)(2,1)S(1)} %get-tuple-element.10) | copy-start | bytes 4718596
  301.9 6.4 %copy-start.9 = (bf16[128,2,6,512]{3,0,2,1:T(8,128)(2,1)}, bf16[128,2,6,512]{3,0,2,1:T(8,128)(2,1)S(1)}, u32[]{:S(2)}) copy-start(bf16[128,2,6,512]{3,0,2,1:T(8,128)(2,1)S(1)} %get-tuple-element.9) | copy-start | bytes 4718596
  322.9 19.3 %slice-start.4 = ((s8[6291456]{0:T(1024)(128)(4,1)}), s8[2097152]{0:T(1024)(128)(4,1)S(1)}, s32[]{:S(2)}) async-start(s8[6291456]{0:T(1024)(128)(4,1)} %bitcast.130), calls=%async_computation.9 | async-start | bytes 4194304
  322.9 111.5 %all-to-all-start.2 = ((bf16[128,12,2048]{2,1,0:T(8,128)(2,1)}), bf16[128,12,2048]{2,1,0:T(8,128)(2,1)}, u32[]{:S(2)}, u32[]{:S(2)}) async-start(bf16[128,12,2048]{2,1,0:T(8,128)(2,1)} %copy.42), calls=%async_computation.2 | async-start | bytes 16777216 | tf_op jit(solution)/shard_map/all_to_all | solution.py:125
  333.3 8.9 %slice-start.5 = ((s8[6291456]{0:T(1024)(128)(4,1)}), s8[4194304]{0:T(1024)(128)(4,1)S(1)}, s32[]{:S(2)}) async-start(s8[6291456]{0:T(1024)(128)(4,1)} %bitcast.130), calls=%async_computation.10 | async-start | bytes 8388608
  333.3 8.9 %copy-start.8 = (bf16[128,2,6,512]{3,0,2,1:T(8,128)(2,1)S(1)}, bf16[128,2,6,512]{3,0,2,1:T(8,128)(2,1)}, u32[]{:S(2)}) copy-start(bf16[128,2,6,512]{3,0,2,1:T(8,128)(2,1)} %copy-done.7) | copy-start | bytes 4718596
  333.3 14.0 %slice-start.2 = ((s8[6291456]{0:T(1024)(128)(4,1)}), s8[4194304]{0:T(1024)(128)(4,1)S(1)}, s32[]{:S(2)}) async-start(s8[6291456]{0:T(1024)(128)(4,1)} %bitcast.124), calls=%async_computation.7 | async-start | bytes 8388608
  342.2 5.1 slice-start.3
  470.0 9.9 %copy-start.1 = (bf16[1,128,2048]{2,1,0:T(8,128)(2,1)S(1)}, bf16[1,128,2048]{2,1,0:T(8,128)(2,1)}, u32[]{:S(2)}) copy-start(bf16[1,128,2048]{2,1,0:T(8,128)(2,1)} %param.8) | copy-start | bytes 1572868
  470.0 9.9 %copy-start.11 = (f32[16,1,128]{2,1,0:T(1,128)S(1)}, f32[16,1,128]{2,1,0:T(1,128)}, u32[]{:S(2)}) copy-start(f32[16,1,128]{2,1,0:T(1,128)} %copy-done.10) | copy-start | bytes 24580
  470.1 9.9 %copy-start.14 = (f32[128]{0:T(128)S(1)}, f32[128]{0:T(128)}, u32[]{:S(2)}) copy-start(f32[128]{0:T(128)} %copy-done.13) | copy-start | bytes 1540
  470.1 33.0 %copy-start.6 = (bf16[1,128,2048]{2,1,0:T(8,128)(2,1)S(1)}, bf16[1,128,2048]{2,1,0:T(8,128)(2,1)}, u32[]{:S(2)}) copy-start(bf16[1,128,2048]{2,1,0:T(8,128)(2,1)} %param.9) | copy-start | bytes 1572868
  480.9 15.9 %all-to-all-start.3 = ((f32[16,1,128]{2,1,0:T(1,128)}), f32[16,1,128]{2,1,0:T(1,128)S(1)}, u32[]{:S(2)}, u32[]{:S(2)}) async-start(f32[16,1,128]{2,1,0:T(1,128)} %bitcast.18), calls=%async_computation.3 | async-start | bytes 16384 | tf_op jit(solution)/shard_map/all_to_all | solution.py:47
  497.4 10.2 %all-to-all-start.4 = ((f32[8,1,128]{2,1,0:T(1,128)}), f32[8,1,128]{2,1,0:T(1,128)S(1)}, u32[]{:S(2)}, u32[]{:S(2)}) async-start(f32[8,1,128]{2,1,0:T(1,128)} %broadcast_in_dim.51), calls=%async_computation.4 | async-start | bytes 8192 | tf_op jit(solution)/shard_map/all_to_all | solution.py:20
where the time goes:
time: 519 us; the launch traced here: 509 us
  blocking collectives  155 us (30%)
  local copies, waits for them, and re-layouts  139 us (27%)
  waiting for transfers between devices  88.6 us (17%)
  matrix products  58.6 us (11%)
  other arithmetic  33.4 us (6%)
  starting transfers between devices  33.1 us (6%)
    all_to_all x1, blocking collectives, sent_together(): lax.all_to_all(both, axis, split_axis=split_dim, concat_axis=concat_dim,...  155 us
    all_to_all x1, waiting for transfers between devices, shards(): lax.all_to_all(returned.reshape(flat_shape), ('dp', 'seq'), split_axis=0,...  78.8 us
    gather x2, local copies, waits for them, and re-layouts, shards(): weighted[source]  26.5 us
    mul x3, local copies, waits for them, and re-layouts, shards(): route_weights[0][:, :, None] * upstream[:, None, :].astype(jnp.float32)  22 us
    slice x3, local copies, waits for them, and re-layouts, sent_together(): done.append(lax.slice_in_dim(out, at, at + a.shape[along], axis=along))  21.5 us
    gather x2, local copies, waits for them, and re-layouts, shards(): normed[source // TOP]  17.7 us
    gather x1, local copies, waits for them, and re-layouts, shards(): back_flat[slot_index].astype(jnp.float32)  14.4 us
    all_to_all x2, starting transfers between devices, from_everyone(): lax.all_to_all(jnp.broadcast_to(x[None], (peers, *x.shape)), axis, 0, 0,...  13.2 us
  transfers between devices with their start and end apart: 4, of which 3 were waited for; matrix products, arithmetic and copies ran while one was open for 17% of the time, Pallas kernels for 0%

commit v1 on v0

v1 whole, which is shorter than its diff:
```python
import functools

import jax
import jax.numpy as jnp
import numpy as np
from jax import lax
from jax.experimental import pallas as pl
from jax.experimental.pallas import tpu as pltpu
from jax.sharding import PartitionSpec as P

TOP = 10
EPSILON = 1e-06
CAP = 6
BF = jnp.bfloat16
F32 = jnp.float32
VMEM_LIMIT = 60 * 2**20


def dot(a, b, ca=1, cb=0):
    return lax.dot_general(a, b, (((ca,), (cb,)), ((), ())), preferred_element_type=F32)


def dispatch_kernel(which, ids_ref, w_ref, hid_ref, cot_ref, send_ref, tab_ref, tab_s, wt_s, src_s):
    step = pl.program_id(0)
    tokens = hid_ref.shape[0]
    half = hid_ref.shape[1] // 2
    devices = tab_s.shape[0]

    @pl.when(step == 0)
    def _():
        expert = 2 * lax.broadcasted_iota(jnp.int32, (devices, tokens), 0) + which
        hit = jnp.zeros((devices, tokens), F32)
        weight = jnp.zeros((devices, tokens), F32)
        for k in range(TOP):
            same = ids_ref[k : k + 1, :] == expert
            hit = hit + jnp.where(same, 1.0, 0.0)
            weight = weight + jnp.where(same, w_ref[k : k + 1, :], 0.0)
        earlier = lax.broadcasted_iota(jnp.int32, (tokens, tokens), 0) < lax.broadcasted_iota(
            jnp.int32, (tokens, tokens), 1
        )
        rank = dot(hit.astype(BF), jnp.where(earlier, 1.0, 0.0).astype(BF))
        table = jnp.where(hit > 0.0, rank, -1.0)
        tab_s[...] = table
        tab_ref[...] = table.astype(BF)
        wt_s[...] = weight
        for h in range(2):
            src_s[h * 2 * tokens : h * 2 * tokens + tokens, :] = hid_ref[:, h * half : (h + 1) * half]
            src_s[h * 2 * tokens + tokens : (h + 1) * 2 * tokens, :] = cot_ref[:, h * half : (h + 1) * half]

    group = send_ref.shape[0] // 24
    at = pl.ds(pl.multiple_of(step * group, group), group)
    shape = (group, 24, tokens)
    table = jnp.broadcast_to(tab_s[at, :][:, None, :], shape)
    weight = jnp.broadcast_to(wt_s[at, :][:, None, :], shape)
    row = lax.broadcasted_iota(jnp.int32, shape, 1)
    in_half = jnp.where(row >= 12, 1, 0)
    row = row - 12 * in_half
    is_grad = jnp.where(row >= CAP, 1, 0)
    slot = (row - CAP * is_grad).astype(F32)
    flat = (group * 24, tokens)
    pick = jnp.where(table == slot, 1.0, 0.0)
    scale = jnp.sum(
        jnp.where(is_grad == 1, pick * weight, jnp.where(lax.broadcasted_iota(jnp.int32, shape, 2) == 0, 1.0, 0.0)),
        axis=2,
        keepdims=True,
    ).reshape(flat[0], 1)
    kind = 2 * in_half + is_grad
    pieces = [jnp.where(kind == m, pick, 0.0).reshape(flat).astype(BF) for m in range(4)]
    left = jnp.concatenate(pieces, axis=1)
    send_ref[...] = (dot(left, src_s[...]) * scale).astype(BF)


def dispatch(which, devices, ids_t, w_t, hidden, cot):
    tokens, width = hidden.shape
    steps = 8
    rows = devices * 24
    whole = lambda *s: pl.BlockSpec(s, lambda g: tuple(0 for _ in s))
    return pl.pallas_call(
        functools.partial(dispatch_kernel, which),
        grid=(steps,),
        out_shape=[
            jax.ShapeDtypeStruct((rows, width // 2), BF),
            jax.ShapeDtypeStruct((devices, tokens), BF),
        ],
        in_specs=[whole(TOP, tokens), whole(TOP, tokens), whole(tokens, width), whole(tokens, width)],
        out_specs=[pl.BlockSpec((rows // steps, width // 2), lambda g: (g, 0)), whole(devices, tokens)],
        scratch_shapes=[
            pltpu.VMEM((devices, tokens), F32),
            pltpu.VMEM((devices, tokens), F32),
            pltpu.VMEM((4 * tokens, width // 2), BF),
        ],
        compiler_params=pltpu.CompilerParams(vmem_limit_bytes=32 * 2**20),
        cost_estimate=pl.CostEstimate(flops=8 * 10**9, bytes_accessed=8 * 10**6, transcendentals=0),
        name=f"dispatch{which}",
    )(ids_t, w_t, hidden, cot)


def order_in():
    m = np.zeros((192, 192), np.float32)
    for s in range(8):
        for h in range(2):
            for a in range(2):
                for r in range(CAP):
                    m[a * 96 + h * 48 + s * CAP + r, s * 24 + h * 12 + a * CAP + r] = 1
    return m


def order_out():
    m = np.zeros((192, 192), np.float32)
    for s in range(8):
        for q in range(4):
            for r in range(CAP):
                m[s * 24 + q * CAP + r, q * 48 + s * CAP + r] = 1
    return m


def expert_kernel(
    first, rows_ref, into_ref, out_of_ref, gain_ref, gate_ref, up_ref, down_ref, *refs
):
    refs = refs if first else refs[5:]
    send_ref, norm_ref, grad_ref, act_ref, gb_ref, ub_ref, sum_ref, raw_s = refs
    rows = raw_s.shape[0]
    width = raw_s.shape[1]
    half, quarter = width // 2, width // 4
    subs = rows // 48
    for b in range(subs):
        moved = dot(into_ref[...], rows_ref[b * 192 : (b + 1) * 192, :])
        for h in range(2):
            raw_s[b * 48 : (b + 1) * 48, h * half : (h + 1) * half] = moved[h * 48 : (h + 1) * 48, :]
            grad_ref[0, b * 48 : (b + 1) * 48, h * half : (h + 1) * half] = moved[
                96 + h * 48 : 96 + (h + 1) * 48, :
            ].astype(BF)
    raw = raw_s[...]
    root = lax.rsqrt(jnp.mean(raw * raw, axis=1, keepdims=True) + EPSILON)
    scaled = raw * root
    normed = (scaled * gain_ref[...]).astype(BF)
    norm_ref[0] = normed
    pre_gate = dot(normed, gate_ref[0])
    pre_up = dot(normed, up_ref[0])
    sig = jax.nn.sigmoid(pre_gate)
    silu = pre_gate * sig
    act_ref[0] = (silu * pre_up).astype(BF)
    grad_act = dot(grad_ref[0], down_ref[0], 1, 1)
    gate_back = (grad_act * pre_up * sig * (1.0 + pre_gate * (1.0 - sig))).astype(BF)
    up_back = (grad_act * silu).astype(BF)
    gb_ref[0] = gate_back
    ub_ref[0] = up_back
    returned = (dot(gate_back, gate_ref[0], 1, 1) + dot(up_back, up_ref[0], 1, 1)).astype(BF)
    partial = jnp.sum(returned.astype(F32) * (raw_s[...] * root), axis=0, keepdims=True)

    @pl.when(pl.program_id(0) == 0)
    def _():
        sum_ref[...] = jnp.zeros_like(sum_ref)

    sum_ref[...] += partial
    for b in range(subs):
        part = returned[b * 48 : (b + 1) * 48, :]
        stacked = jnp.concatenate([part[:, q * quarter : (q + 1) * quarter] for q in range(4)], axis=0)
        send_ref[b * 192 : (b + 1) * 192, :] = dot(out_of_ref[...], stacked).astype(BF)


def expert(which, arrived, gain, gate, up, down, kept):
    total, half = arrived.shape
    width = 2 * half
    hidden = gate.shape[2]
    experts = gate.shape[0]
    slots = total // 4
    steps = 4
    rows = slots // steps
    whole = lambda *s: pl.BlockSpec(s, lambda g: tuple(0 for _ in s))
    mine = lambda *s: pl.BlockSpec((1, *s), lambda g: (which, 0, 0))
    ours = lambda *s: pl.BlockSpec((1, *s), lambda g: (which, g, 0))
    first = kept is None
    keep_shapes = [(experts, slots, width)] * 2 + [(experts, slots, hidden)] * 3
    keep_specs = [ours(rows, width)] * 2 + [ours(rows, hidden)] * 3
    operands = [
        arrived,
        jnp.asarray(order_in(), BF),
        jnp.asarray(order_out(), BF),
        gain,
        gate,
        up,
        down,
    ]
    in_specs = [
        pl.BlockSpec((rows * 4, half), lambda g: (g, 0)),
        whole(192, 192),
        whole(192, 192),
        whole(1, width),
        mine(width, hidden),
        mine(width, hidden),
        mine(hidden, width),
    ]
    aliases = {}
    if not first:
        aliases = {len(operands) + n: 1 + n for n in range(5)}
        operands += list(kept)
        in_specs += [pl.BlockSpec(memory_space=pl.ANY)] * 5
    outs = pl.pallas_call(
        functools.partial(expert_kernel, first),
        grid=(steps,),
        out_shape=[jax.ShapeDtypeStruct((total, width // 4), BF)]
        + [jax.ShapeDtypeStruct(s, BF) for s in keep_shapes]
        + [jax.ShapeDtypeStruct((1, width), F32)],
        in_specs=in_specs,
        out_specs=[pl.BlockSpec((rows * 4, width // 4), lambda g: (g, 0))] + keep_specs + [whole(1, width)],
        scratch_shapes=[pltpu.VMEM((rows, width), F32)],
        input_output_aliases=aliases,
        compiler_params=pltpu.CompilerParams(vmem_limit_bytes=VMEM_LIMIT),
        cost_estimate=pl.CostEstimate(flops=25 * 10**9, bytes_accessed=22 * 10**6, transcendentals=10**6),
        name=f"expert{which}",
    )(*operands)
    return outs[0], outs[1:6], outs[6]


def combine_kernel(last, tab_ref, rows_ref, slot_ref, part_ref, *refs):
    if last:
        prev_ref, hid_ref, cot_ref, gain_ref, out_ref, acc = refs
    else:
        out_ref, acc = refs
    step = pl.program_id(0)
    count = rows_ref.shape[0]
    group, tokens = tab_ref.shape
    quarter = rows_ref.shape[1]

    @pl.when(step == 0)
    def _():
        acc[...] = jnp.zeros_like(acc)

    at = lax.broadcasted_iota(jnp.int32, (group, count), 1) - 24 * lax.broadcasted_iota(
        jnp.int32, (group, count), 0
    )
    spread = jnp.where((at >= 0) & (at < 24), 1.0, 0.0).astype(BF)
    table = dot(tab_ref[...], spread, 0, 0)
    pick = jnp.where(table == slot_ref[...], 1.0, 0.0)
    left = jnp.concatenate(
        [jnp.where(part_ref[...] == float(q), pick, 0.0).astype(BF) for q in range(4)], axis=0
    )
    acc[...] += dot(left, rows_ref[...])

    @pl.when(step == pl.num_programs(0) - 1)
    def _():
        summed = jnp.concatenate([acc[q * tokens : (q + 1) * tokens, :] for q in range(4)], axis=1)
        if not last:
            out_ref[...] = summed
        else:
            summed = summed + prev_ref[...]
            raw = hid_ref[...].astype(F32)
            root = lax.rsqrt(jnp.mean(raw * raw, axis=1, keepdims=True) + EPSILON)
            scaled = raw * root
            gained = summed * gain_ref[...]
            centre = jnp.mean(gained * scaled, axis=1, keepdims=True)
            out_ref[...] = (cot_ref[...].astype(F32) + root * (gained - scaled * centre)).astype(BF)


def combine(which, table, back, tokens, extra):
    total, quarter = back.shape
    width = 4 * quarter
    devices = table.shape[0]
    steps = 8
    group = devices // steps
    place = np.arange(group * 24) % 24
    slot = jnp.asarray((place % CAP)[None, :], F32)
    part = jnp.asarray((place // CAP)[None, :], F32)
    whole = lambda *s: pl.BlockSpec(s, lambda g: tuple(0 for _ in s))
    last = len(extra) > 0
    extra_specs = [whole(*e.shape) for e in extra]
    return pl.pallas_call(
        functools.partial(combine_kernel, last),
        grid=(steps,),
        out_shape=jax.ShapeDtypeStruct((tokens, width), BF if last else F32),
        in_specs=[
            pl.BlockSpec((group, tokens), lambda g: (g, 0)),
            pl.BlockSpec((group * 24, quarter), lambda g: (g, 0)),
            whole(1, group * 24),
            whole(1, group * 24),
        ]
        + extra_specs,
        out_specs=whole(tokens, width),
        scratch_shapes=[pltpu.VMEM((4 * tokens, quarter), F32)],
        compiler_params=pltpu.CompilerParams(vmem_limit_bytes=32 * 2**20),
        cost_estimate=pl.CostEstimate(flops=4 * 10**9, bytes_accessed=6 * 10**6, transcendentals=0),
        name=f"combine{which}",
    )(table, back, slot, part, *extra)


def exchanged(x, devices):
    rows, columns = x.shape
    out = lax.all_to_all(x.reshape(devices, rows // devices, columns), ("dp", "seq"), 0, 0, tiled=True)
    return out.reshape(rows, columns)


def from_everyone(x, axis):
    peers = lax.axis_size(axis)
    return lax.all_to_all(jnp.broadcast_to(x[None], (peers, *x.shape)), axis, 0, 0, tiled=True)


def shards(
    hidden_in, cotangent, norm_gain, route_weights, expert_ids, expert_gate, expert_up, expert_down
):
    hidden, cot = hidden_in[0], cotangent[0]
    tokens, width = hidden.shape
    devices = lax.axis_size("dp") * lax.axis_size("seq")
    ids_t = expert_ids[0].T
    w_t = route_weights[0].T
    gain = from_everyone(norm_gain, "dp").reshape(1, width)
    sent0, table0 = dispatch(0, devices, ids_t, w_t, hidden, cot)
    sent1, table1 = dispatch(1, devices, ids_t, w_t, hidden, cot)
    came0 = exchanged(sent0, devices)
    came1 = exchanged(sent1, devices)
    ret0, kept, sum0 = expert(0, came0, gain, expert_gate, expert_up, expert_down, None)
    back0 = exchanged(ret0, devices)
    ret1, kept, sum1 = expert(1, came1, gain, expert_gate, expert_up, expert_down, kept)
    back1 = exchanged(ret1, devices)
    normed, grads, act, gate_back, up_back = kept
    outer = lambda a, b: jnp.einsum("era,erb->eab", a, b, preferred_element_type=F32).astype(BF)
    grad_down = outer(act, grads)
    grad_gate = outer(normed, gate_back)
    grad_up = outer(normed, up_back)
    local_gain = (sum0 + sum1).reshape(lax.axis_size("dp"), -1)
    share = jnp.sum(lax.all_to_all(local_gain, "dp", 0, 0, tiled=True), axis=0)
    grad_gain = jnp.sum(from_everyone(share, "seq"), axis=0)
    part0 = combine(0, table0, back0, tokens, ())
    grad_hidden = combine(1, table1, back1, tokens, (part0, hidden, cot, gain))
    return grad_hidden[None], grad_gain, grad_gate, grad_up, grad_down


def solution(mesh):
    rows = P("dp", "seq", None)
    experts = P(("dp", "seq"), None, None)
    return jax.shard_map(
        shards,
        mesh=mesh,
        in_specs=(rows, rows, P("dp"), rows, rows, experts, experts, experts),
        out_specs=(rows, P("dp"), experts, experts, experts),
        check_vma=False,
    )
```

time: 519 us -> 343 us (0.66); the launches traced: 509 us -> 342 us
  local copies, waits for them, and re-layouts: 139 us -> 16.9 us
  blocking collectives: 155 us -> 68.8 us
  Pallas kernels: 0 us -> 63.7 us
  waiting for transfers between devices: 88.6 us -> 134 us
  matrix products: 58.6 us -> 23.4 us
  other arithmetic: 33.4 us -> 1.28 us
    all_to_all x1 -> x3, blocking collectives: 155 us -> 68.8 us  [the longest x1 45.4 us: exchanged(): lax.all_to_all(x.reshape(devices, rows // devices, columns), ('dp', 'seq'...]
    pallas_call x0 -> x6, Pallas kernels: none -> 63.7 us  [the longest x2 42.5 us: expert(): pl.pallas_call(functools.partial(expert_kernel, first), grid=(steps,), ou...]
    gather x5 -> x0, local copies, waits for them, and re-layouts: 58.5 us -> none  [the longest x2 26.5 us: shards(): weighted[source]]
    all_to_all x2 -> x3, waiting for transfers between devices: 85.2 us -> 134 us  [exchanged(): lax.all_to_all(x.reshape(devices, rows // devices, columns), ('dp', 'seq'...]
    dot_general x9 -> x3, matrix products: 58.6 us -> 23.4 us  [shards(): jnp.einsum('era,erb->eab', a, b, preferred_element_type=F32).astype(BF)]
    mul x5 -> x0, local copies, waits for them, and re-layouts: 22.2 us -> none  [the longest x3 22 us: shards(): route_weights[0][:, :, None] * upstream[:, None, :].astype(jnp.float32)]
    slice x3 -> x0, local copies, waits for them, and re-layouts: 21.5 us -> none  [sent_together(): done.append(lax.slice_in_dim(out, at, at + a.shape[along], axis=along))]
    reshape x2 -> x0, local copies, waits for them, and re-layouts: 17.6 us -> none  [the longest x1 10.7 us: shards(): back_flat = back_rows.reshape(expert_count * capacity, model_width)]
  transfers between devices with their start and end apart: 4 -> 4, of which waited for: 3 -> 3; matrix products, arithmetic and copies ran while one was open for 17% -> 7% of each run, Pallas kernels for 0% -> 11%
where the time goes in v1:
time: 343 us; the launch traced here: 342 us
  waiting for transfers between devices  134 us (39%)
  blocking collectives  68.8 us (20%)
  Pallas kernels  63.7 us (19%)
  starting transfers between devices  33.8 us (10%)
  matrix products  23.4 us (7%)
  local copies, waits for them, and re-layouts  16.9 us (5%)
    all_to_all x3, waiting for transfers between devices, exchanged(): lax.all_to_all(x.reshape(devices, rows // devices, columns), ('dp', 'seq'...  134 us
    all_to_all x1, blocking collectives, exchanged(): lax.all_to_all(x.reshape(devices, rows // devices, columns), ('dp', 'seq'...  45.4 us
    pallas_call x2, Pallas kernels, expert(): pl.pallas_call(functools.partial(expert_kernel, first), grid=(steps,), ou...  42.5 us
    all_to_all x3, starting transfers between devices, exchanged(): lax.all_to_all(x.reshape(devices, rows // devices, columns), ('dp', 'seq'...  26.2 us
    dot_general x3, matrix products, shards(): jnp.einsum('era,erb->eab', a, b, preferred_element_type=F32).astype(BF)  23.4 us
    unnamed x44, local copies, waits for them, and re-layouts  15.6 us
    all_to_all x1, blocking collectives, from_everyone(): lax.all_to_all(jnp.broadcast_to(x[None], (peers, *x.shape)), axis, 0, 0,...  11.8 us
    all_to_all x1, blocking collectives, shards(): share = jnp.sum(lax.all_to_all(local_gain, 'dp', 0, 0, tiled=True), axis=0)  11.6 us
  transfers between devices with their start and end apart: 4, of which 3 were waited for; matrix products, arithmetic and copies ran while one was open for 7% of the time, Pallas kernels for 11%

profile of v1, /device:TPU:1, one launch (start us, length us, event | category | flops | bytes accessed | tf_op | source)
XLA Modules:
  0.0 342.4 jit_solution(14329668760249734539)
XLA Ops:
  0.6 1.3 broadcast_in_dim.6
  1.9 7.6 %all-to-all-start.1 = ((f32[16,1,128]{2,1,0:T(1,128)}), f32[16,1,128]{2,1,0:T(1,128)S(1)}, u32[]{:S(2)}, u32[]{:S(2)}) async-start(f32[16,1,128]{2,1,0:T(1,128)} %broadcast_in_dim.6), calls=%async_computation.1 | async-start | bytes 16384 | tf_op jit(solution)/shard_map/all_to_all | solution.py:295
  9.5 0.7 copy.49
  10.2 0.7 copy.50
  10.9 0.0 copy-start.5
  10.9 1.0 copy-done.5
  11.9 0.0 copy-start.8
  11.9 1.0 copy-done.8
  12.9 5.0 %dispatch0.1 = (bf16[3072,1024]{1,0:T(8,128)(2,1)S(1)}, bf16[128,128]{1,0:T(8,128)(2,1)S(1)}) custom-call(s32[10,128]{1,0:T(8,128)S(1)} %bitcast.42, f32[10,128]{1,0:T(8,128)S(1)} %bitcast.40, bf16[128,2048]{1,0:T(8,128)(2,1)S(1)} %bitcast.44, bf16[128,2048]{1,0:T(8,128)(2,1)S(1)} %bitcast.47), custom_call_target="tpu_custom_call" | custom-call | flops 8000000000 | bytes 8000000 | tf_op jit(solution)/shard_map/dispatch0/pallas_call | solution.py:78
  17.9 0.0 copy-start.1
  17.9 2.6 copy-done.1
  20.5 0.0 all-to-all-done.1
  20.5 0.0 copy-start.3
  20.5 0.0 copy-start.6
  20.5 0.0 copy-start.9
  20.6 0.6 copy-done.3
  21.1 11.5 %all-to-all-start.2 = ((bf16[128,24,1024]{2,1,0:T(8,128)(2,1)}), bf16[128,24,1024]{2,1,0:T(8,128)(2,1)}, u32[]{:S(2)}, u32[]{:S(2)}) async-start(bf16[128,24,1024]{2,1,0:T(8,128)(2,1)} %bitcast.34), calls=%async_computation.2 | async-start | bytes 12582912 | tf_op jit(solution)/shard_map/all_to_all | solution.py:289
  32.7 0.0 copy-done.6
  32.7 0.0 copy-done.9
  32.7 5.0 %dispatch1.1 = (bf16[3072,1024]{1,0:T(8,128)(2,1)S(1)}, bf16[128,128]{1,0:T(8,128)(2,1)S(1)}) custom-call(s32[10,128]{1,0:T(8,128)S(1)} %bitcast.43, f32[10,128]{1,0:T(8,128)S(1)} %bitcast.41, bf16[128,2048]{1,0:T(8,128)(2,1)S(1)} %bitcast.45, bf16[128,2048]{1,0:T(8,128)(2,1)S(1)} %bitcast.48), custom_call_target="tpu_custom_call" | custom-call | flops 8000000000 | bytes 8000000 | tf_op jit(solution)/shard_map/dispatch1/pallas_call | solution.py:78
  37.7 0.0 copy-start
  37.7 2.7 copy-done
  40.3 68.8 %all-to-all-done.2 = bf16[128,24,1024]{2,1,0:T(8,128)(2,1)} async-done(((bf16[128,24,1024]{2,1,0:T(8,128)(2,1)}), bf16[128,24,1024]{2,1,0:T(8,128)(2,1)}, u32[]{:S(2)}, u32[]{:S(2)}) %all-to-all-start.2) | async-done | bytes 6291488 | tf_op jit(solution)/shard_map/all_to_all | solution.py:289
  109.2 9.7 %all-to-all-start = ((bf16[128,24,1024]{2,1,0:T(8,128)(2,1)}), bf16[128,24,1024]{2,1,0:T(8,128)(2,1)}, u32[]{:S(2)}, u32[]{:S(2)}) async-start(bf16[128,24,1024]{2,1,0:T(8,128)(2,1)} %bitcast.33), calls=%async_computation | async-start | bytes 12582912 | tf_op jit(solution)/shard_map/all_to_all | solution.py:289
  118.9 21.2 %expert0.1 = (bf16[3072,512]{1,0:T(8,128)(2,1)}, bf16[2,768,2048]{2,1,0:T(8,128)(2,1)}, bf16[2,768,2048]{2,1,0:T(8,128)(2,1)}, bf16[2,768,512]{2,1,0:T(8,128)(2,...) custom-call(bf16[3072,1024]{1,0:T(8,128)(2,1)} %bitcast.8.rows_ref, ...), custom_call_target="tpu_custom_call" | custom-call | flops 24999999488 | bytes 22000000 | tf_op jit(solution)/shard_map/expert0/pallas_call | solution.py:199
  140.1 55.3 %all-to-all-done = bf16[128,24,1024]{2,1,0:T(8,128)(2,1)} async-done(((bf16[128,24,1024]{2,1,0:T(8,128)(2,1)}), bf16[128,24,1024]{2,1,0:T(8,128)(2,1)}, u32[]{:S(2)}, u32[]{:S(2)}) %all-to-all-start) | async-done | bytes 6291488 | tf_op jit(solution)/shard_map/all_to_all | solution.py:289
  195.4 0.0 copy-start.16
  195.4 0.0 copy-start.15
  195.4 21.3 %expert1.1 = (bf16[3072,512]{1,0:T(8,128)(2,1)}, bf16[2,768,2048]{2,1,0:T(8,128)(2,1)}, bf16[2,768,2048]{2,1,0:T(8,128)(2,1)}, bf16[2,768,512]{2,1,0:T(8,128)(2,...) custom-call(bf16[3072,1024]{1,0:T(8,128)(2,1)} %bitcast.5.rows_ref, ...), custom_call_target="tpu_custom_call", output_to_operand_aliasing={{1}: (7, {}), {2}: (8, {}), {3}: (9, {}), {4}: (10, {}), {5... | custom-call | flops 24999999488 | bytes 22000000 | tf_op jit(solution)/shard_map/expert1/pallas_call | solution.py:199
  216.8 0.0 copy-done.16
  216.8 0.7 add_bitcast_fusion
  217.5 11.6 %all_to_all.41 = f32[16,1,128]{2,1,0:T(1,128)S(1)} all-to-all(f32[16,1,128]{2,1,0:T(1,128)S(1)} %add_bitcast_fusion), channel_id=1, replica_groups=mesh['dp'=16,'seq'=8] {'dp'}, dimensions={0} | all-to-all | bytes 16384 | tf_op jit(solution)/shard_map/all_to_all | solution.py:321
  229.1 11.8 %all_to_all.42 = f32[8,1,128]{2,1,0:T(1,128)S(1)} all-to-all(f32[8,1,128]{2,1,0:T(1,128)S(1)} %broadcast_in_dim.8), channel_id=1, replica_groups=mesh['dp'=16,'seq'=8] {'seq'}, dimensions={0} | all-to-all | bytes 8192 | tf_op jit(solution)/shard_map/all_to_all | solution.py:295
  240.9 0.0 copy-done.15
  240.9 45.4 %all_to_all.43 = bf16[128,24,512]{2,1,0:T(8,128)(2,1)} all-to-all(bf16[128,24,512]{2,1,0:T(8,128)(2,1)S(1)} %bitcast.51), channel_id=1, replica_groups=mesh['dp'=16,'seq'=8] {'dp','seq'}, dimensions={0} | all-to-all | bytes 6291456 | tf_op jit(solution)/shard_map/all_to_all | solution.py:289
  286.4 5.0 %all-to-all-start.3 = ((bf16[128,24,512]{2,1,0:T(8,128)(2,1)}), bf16[128,24,512]{2,1,0:T(8,128)(2,1)S(1)}, u32[]{:S(2)}, u32[]{:S(2)}) async-start(bf16[128,24,512]{2,1,0:T(8,128)(2,1)} %bitcast.50), calls=%async_computation.3 | async-start | bytes 6291456 | tf_op jit(solution)/shard_map/all_to_all | solution.py:289
  291.4 0.0 copy-start.17
  291.4 0.0 slice-start
  291.4 8.9 %convolution_convert_fusion.2 = bf16[2,2048,512]{2,1,0:T(8,128)(2,1)} fusion(bf16[2,768,2048]{2,1,0:T(8,128)(2,1)} %get-tuple-element.36, bf16[2,768,512]{2,1,0:T(8,128)(2,1)} %get-tuple-element.37), kind=kOutput, calls=%fused_computation.2 | convolution fusion | flops 3223322624 | bytes 12058624 | tf_op jit(solution)/shard_map/era,erb->eab/dot_general | solution.py:316
  300.3 0.0 copy-done.17
  300.3 0.0 slice-start.1
  300.3 0.0 copy-start.18
  300.3 9.4 %convolution_convert_fusion.1 = bf16[2,2048,512]{2,1,0:T(8,128)(2,1)} fusion(bf16[2,768,2048]{2,1,0:T(8,128)(2,1)} %get-tuple-element.36, bf16[2,768,512]{2,1,0:T(8,128)(2,1)S(1)} %copy-done.17), kind=kOutput, calls=%fused_computation.1 | convolution fusion | flops 3223322624 | bytes 12058624 | tf_op jit(solution)/shard_map/era,erb->eab/dot_general | solution.py:316
  309.7 0.0 slice-done
  309.7 0.0 slice-done.1
  309.7 0.0 copy-done.18
  309.7 0.0 copy-start.11
  309.8 0.0 copy-start.12
  309.8 5.1 %convolution_convert_fusion = bf16[2,512,2048]{2,1,0:T(8,128)(2,1)} fusion(bf16[2,768,512]{2,1,0:T(8,128)(2,1)S(1)} %copy-done.18, bf16[2,768,2048]{2,1,0:T(8,128)(2,1)S(1)} %bitcast.55), kind=kOutput, calls=%fused_computation | convolution fusion | flops 3223322624 | bytes 12058624 | tf_op jit(solution)/shard_map/era,erb->eab/dot_general | solution.py:316
  314.9 0.5 reduce_sum.19
  315.4 0.0 copy-done.11
  315.4 0.0 copy-done.12
  315.4 0.0 copy-start.2
  315.4 1.9 copy-done.2
  317.3 0.0 copy-start.4
  317.3 4.9 %combine0.1.refs_0_ = f32[128,2048]{1,0:T(8,128)S(1)} custom-call(bf16[128,128]{1,0:T(8,128)(2,1)S(1)} %get-tuple-element.32.tab_ref, bf16[3072,512]{1,0:T(8,128)(2,1)S(1)} %bitcast.36, f32[1,384]{1,0:T(1,128)S(1)} %copy-done.12, f32[1,384]{1,0:T(1,128)S(1)} %copy-done.11), custom_call_target="tpu_custom_call" | custom-call | flops 4000000000 | bytes 6000000 | tf_op jit(solution)/shard_map/combine0/pallas_call | solution.py:268
  322.2 0.0 copy-start.13
  322.2 1.0 copy-done.13
  323.2 9.5 %all-to-all-done.3 = bf16[128,24,512]{2,1,0:T(8,128)(2,1)S(1)} async-done(((bf16[128,24,512]{2,1,0:T(8,128)(2,1)}), bf16[128,24,512]{2,1,0:T(8,128)(2,1)S(1)}, u32[]{:S(2)}, u32[]{:S(2)}) %all-to-all-start.3) | async-done | bytes 3145760 | tf_op jit(solution)/shard_map/all_to_all | solution.py:289
  332.7 0.0 copy-done.4
  332.7 1.0 copy-done.7
  333.8 1.0 copy-done.10
  334.8 1.2 copy-done.14
  336.0 6.3 %combine1.1 = bf16[128,2048]{1,0:T(8,128)(2,1)} custom-call(bf16[128,128]{1,0:T(8,128)(2,1)S(1)} %get-tuple-element.23.tab_ref, bf16[3072,512]{1,0:T(8,128)(2,1)S(1)} %bitcast.35, f32[1,384]{1,0:T(1,128)S(1)} %copy-done.12, f32[1,384]{1,0:T(1,128)S(1)} %copy-done.11, f32[128,2048]{1,0:T(8,128)S(1)} %copy-done.14, bf16[128,2048]{1,0:T(8,128)(2,1)S(1)} %bitcast.46, ...), custom_call_target="tpu_custom_call" | custom-call | flops 4000000000 | bytes 6000000 | tf_op jit(solution)/shard_map/combine1/pallas_call | solution.py:268
  (6 shorter events, 0.0 us)
Async XLA Ops:
  1.9 18.7 %all-to-all-start.1 = ((f32[16,1,128]{2,1,0:T(1,128)}), f32[16,1,128]{2,1,0:T(1,128)S(1)}, u32[]{:S(2)}, u32[]{:S(2)}) async-start(f32[16,1,128]{2,1,0:T(1,128)} %broadcast_in_dim.6), calls=%async_computation.1 | async-start | bytes 16384 | tf_op jit(solution)/shard_map/all_to_all | solution.py:295
  10.9 1.0 copy-start.5
  11.9 1.0 copy-start.8
  17.9 2.6 copy-start.1
  20.5 0.6 copy-start.3
  20.5 12.1 %copy-start.6 = (bf16[1,128,2048]{2,1,0:T(8,128)(2,1)S(1)}, bf16[1,128,2048]{2,1,0:T(8,128)(2,1)}, u32[]{:S(2)}) copy-start(bf16[1,128,2048]{2,1,0:T(8,128)(2,1)} %param.16) | copy-start | bytes 1572868
  20.5 12.1 %copy-start.9 = (bf16[1,128,2048]{2,1,0:T(8,128)(2,1)S(1)}, bf16[1,128,2048]{2,1,0:T(8,128)(2,1)}, u32[]{:S(2)}) copy-start(bf16[1,128,2048]{2,1,0:T(8,128)(2,1)} %param.17) | copy-start | bytes 1572868
  21.1 88.0 %all-to-all-start.2 = ((bf16[128,24,1024]{2,1,0:T(8,128)(2,1)}), bf16[128,24,1024]{2,1,0:T(8,128)(2,1)}, u32[]{:S(2)}, u32[]{:S(2)}) async-start(bf16[128,24,1024]{2,1,0:T(8,128)(2,1)} %bitcast.34), calls=%async_computation.2 | async-start | bytes 12582912 | tf_op jit(solution)/shard_map/all_to_all | solution.py:289
  37.7 2.7 copy-start
  109.2 86.2 %all-to-all-start = ((bf16[128,24,1024]{2,1,0:T(8,128)(2,1)}), bf16[128,24,1024]{2,1,0:T(8,128)(2,1)}, u32[]{:S(2)}, u32[]{:S(2)}) async-start(bf16[128,24,1024]{2,1,0:T(8,128)(2,1)} %bitcast.33), calls=%async_computation | async-start | bytes 12582912 | tf_op jit(solution)/shard_map/all_to_all | solution.py:289
  195.4 21.4 %copy-start.16 = (f32[1,2048]{1,0:T(1,128)S(1)}, f32[1,2048]{1,0:T(1,128)}, u32[]{:S(2)}) copy-start(f32[1,2048]{1,0:T(1,128)} %get-tuple-element.34) | copy-start | bytes 24580
  195.4 45.5 %copy-start.15 = (bf16[3072,512]{1,0:T(8,128)(2,1)S(1)}, bf16[3072,512]{1,0:T(8,128)(2,1)}, u32[]{:S(2)}) copy-start(bf16[3072,512]{1,0:T(8,128)(2,1)} %get-tuple-element.33) | copy-start | bytes 9437188
  286.4 46.4 %all-to-all-start.3 = ((bf16[128,24,512]{2,1,0:T(8,128)(2,1)}), bf16[128,24,512]{2,1,0:T(8,128)(2,1)S(1)}, u32[]{:S(2)}, u32[]{:S(2)}) async-start(bf16[128,24,512]{2,1,0:T(8,128)(2,1)} %bitcast.50), calls=%async_computation.3 | async-start | bytes 6291456 | tf_op jit(solution)/shard_map/all_to_all | solution.py:289
  291.4 8.9 %copy-start.17 = (bf16[2,768,512]{2,1,0:T(8,128)(2,1)S(1)}, bf16[2,768,512]{2,1,0:T(8,128)(2,1)}, u32[]{:S(2)}) copy-start(bf16[2,768,512]{2,1,0:T(8,128)(2,1)} %get-tuple-element.38) | copy-start | bytes 4718596
  291.4 18.3 %slice-start = ((s8[6291456]{0:T(1024)(128)(4,1)}), s8[4194304]{0:T(1024)(128)(4,1)S(1)}, s32[]{:S(2)}) async-start(s8[6291456]{0:T(1024)(128)(4,1)} %bitcast.54), calls=%async_computation.7 | async-start | bytes 8388608
  300.3 9.4 %slice-start.1 = ((s8[6291456]{0:T(1024)(128)(4,1)}), s8[2097152]{0:T(1024)(128)(4,1)S(1)}, s32[]{:S(2)}) async-start(s8[6291456]{0:T(1024)(128)(4,1)} %bitcast.54), calls=%async_computation.8 | async-start | bytes 4194304
  300.3 9.4 %copy-start.18 = (bf16[2,768,512]{2,1,0:T(8,128)(2,1)S(1)}, bf16[2,768,512]{2,1,0:T(8,128)(2,1)}, u32[]{:S(2)}) copy-start(bf16[2,768,512]{2,1,0:T(8,128)(2,1)} %get-tuple-element.39) | copy-start | bytes 4718596
  309.7 5.7 %copy-start.11 = (f32[1,384]{1,0:T(1,128)S(1)}, f32[1,384]{1,0:T(1,128)}, u32[]{:S(2)}) copy-start(f32[1,384]{1,0:T(1,128)} %constant.13.clone.part_ref) | copy-start | bytes 4612
  309.8 5.7 %copy-start.12 = (f32[1,384]{1,0:T(1,128)S(1)}, f32[1,384]{1,0:T(1,128)}, u32[]{:S(2)}) copy-start(f32[1,384]{1,0:T(1,128)} %constant.12.clone.slot_ref) | copy-start | bytes 4612
  315.4 1.9 copy-start.2
  317.3 15.4 %copy-start.4 = (f32[16,1,128]{2,1,0:T(1,128)S(1)}, f32[16,1,128]{2,1,0:T(1,128)}, u32[]{:S(2)}) copy-start(f32[16,1,128]{2,1,0:T(1,128)} %copy-done.3) | copy-start | bytes 24580
  322.2 1.0 copy-start.13
  332.7 1.0 copy-start.7
  333.8 1.0 copy-start.10
  334.8 1.2 copy-start.14

commit v2 on v1

--- a/solution.py
+++ b/solution.py
@@ -7,6 +7,7 @@
 from jax.experimental import pallas as pl
 from jax.experimental.pallas import tpu as pltpu
 from jax.sharding import PartitionSpec as P
+
 
 TOP = 10
 EPSILON = 1e-06
@@ -91,7 +92,6 @@
         ],
         compiler_params=pltpu.CompilerParams(vmem_limit_bytes=32 * 2**20),
         cost_estimate=pl.CostEstimate(flops=8 * 10**9, bytes_accessed=8 * 10**6, transcendentals=0),
-        name=f"dispatch{which}",
     )(ids_t, w_t, hidden, cot)
 
 
@@ -208,7 +208,6 @@
         input_output_aliases=aliases,
         compiler_params=pltpu.CompilerParams(vmem_limit_bytes=VMEM_LIMIT),
         cost_estimate=pl.CostEstimate(flops=25 * 10**9, bytes_accessed=22 * 10**6, transcendentals=10**6),
-        name=f"expert{which}",
     )(*operands)
     return outs[0], outs[1:6], outs[6]
 
@@ -221,7 +220,6 @@
     step = pl.program_id(0)
     count = rows_ref.shape[0]
     group, tokens = tab_ref.shape
-    quarter = rows_ref.shape[1]
 
     @pl.when(step == 0)
     def _():
@@ -253,8 +251,8 @@
             out_ref[...] = (cot_ref[...].astype(F32) + root * (gained - scaled * centre)).astype(BF)
 
 
-def combine(which, table, back, tokens, extra):
-    total, quarter = back.shape
+def combine(table, back, tokens, extra):
+    _, quarter = back.shape
     width = 4 * quarter
     devices = table.shape[0]
     steps = 8
@@ -280,7 +278,6 @@
         scratch_shapes=[pltpu.VMEM((4 * tokens, quarter), F32)],
         compiler_params=pltpu.CompilerParams(vmem_limit_bytes=32 * 2**20),
         cost_estimate=pl.CostEstimate(flops=4 * 10**9, bytes_accessed=6 * 10**6, transcendentals=0),
-        name=f"combine{which}",
     )(table, back, slot, part, *extra)
 
 
@@ -288,11 +285,6 @@
     rows, columns = x.shape
     out = lax.all_to_all(x.reshape(devices, rows // devices, columns), ("dp", "seq"), 0, 0, tiled=True)
     return out.reshape(rows, columns)
-
-
-def from_everyone(x, axis):
-    peers = lax.axis_size(axis)
-    return lax.all_to_all(jnp.broadcast_to(x[None], (peers, *x.shape)), axis, 0, 0, tiled=True)
 
 
 def shards(
@@ -303,10 +295,10 @@
     devices = lax.axis_size("dp") * lax.axis_size("seq")
     ids_t = expert_ids[0].T
     w_t = route_weights[0].T
-    gain = from_everyone(norm_gain, "dp").reshape(1, width)
+    gain = lax.all_gather(norm_gain, "dp", tiled=True).reshape(1, width)
     sent0, table0 = dispatch(0, devices, ids_t, w_t, hidden, cot)
+    came0 = exchanged(sent0, devices)
     sent1, table1 = dispatch(1, devices, ids_t, w_t, hidden, cot)
-    came0 = exchanged(sent0, devices)
     came1 = exchanged(sent1, devices)
     ret0, kept, sum0 = expert(0, came0, gain, expert_gate, expert_up, expert_down, None)
     back0 = exchanged(ret0, devices)
@@ -317,11 +309,11 @@
     grad_down = outer(act, grads)
     grad_gate = outer(normed, gate_back)
     grad_up = outer(normed, up_back)
-    local_gain = (sum0 + sum1).reshape(lax.axis_size("dp"), -1)
-    share = jnp.sum(lax.all_to_all(local_gain, "dp", 0, 0, tiled=True), axis=0)
-    grad_gain = jnp.sum(from_everyone(share, "seq"), axis=0)
-    part0 = combine(0, table0, back0, tokens, ())
-    grad_hidden = combine(1, table1, back1, tokens, (part0, hidden, cot, gain))
+    everyone = lax.psum((sum0 + sum1).reshape(-1), ("dp", "seq"))
+    share = width // lax.axis_size("dp")
+    grad_gain = lax.dynamic_slice(everyone, (lax.axis_index("dp") * share,), (share,))
+    part0 = combine(table0, back0, tokens, ())
+    grad_hidden = combine(table1, back1, tokens, (part0, hidden, cot, gain))
     return grad_hidden[None], grad_gain, grad_gate, grad_up, grad_down
 
 

time: 343 us -> 410 us (1.20)
  blocking collectives: 68.8 us -> 177 us
  waiting for transfers between devices: 134 us -> 88.8 us
  starting transfers between devices: 33.8 us -> 41.5 us
    psum x0 -> x1, blocking collectives: none -> 93.4 us  [shards(): everyone = lax.psum((sum0 + sum1).reshape(-1), ('dp', 'seq'))]
    all_gather x0 -> x1, blocking collectives: none -> 83.3 us  [shards(): gain = lax.all_gather(norm_gain, 'dp', tiled=True).reshape(1, width)]
    all_to_all x3 -> x0, blocking collectives: 68.8 us -> none  [the longest x1 45.4 us: exchanged(): lax.all_to_all(x.reshape(devices, rows // devices, columns), ('dp', 'seq'...]
    all_to_all x3 -> x4, waiting for transfers between devices: 134 us -> 88.8 us  [exchanged(): lax.all_to_all(x.reshape(devices, rows // devices, columns), ('dp', 'seq'...]
    all_to_all x3 -> x4, starting transfers between devices: 26.2 us -> 41.5 us  [exchanged(): lax.all_to_all(x.reshape(devices, rows // devices, columns), ('dp', 'seq'...]
    all_to_all x1 -> x0, starting transfers between devices: 7.57 us -> none  [from_everyone(): lax.all_to_all(jnp.broadcast_to(x[None], (peers, *x.shape)), axis, 0, 0,...]
    unnamed x44 -> x40, local copies, waits for them, and re-layouts: 15.6 us -> 13.1 us
  transfers between devices with their start and end apart: 4 -> 4, of which waited for: 3 -> 2; matrix products, arithmetic and copies ran while one was open for 7% -> 6% of each run, Pallas kernels for 11% -> 13%
where the time goes in v2:
time: 410 us; the launch traced here: 409 us
  blocking collectives  177 us (43%)
  waiting for transfers between devices  88.8 us (22%)
  Pallas kernels  65.7 us (16%)
  starting transfers between devices  41.5 us (10%)
  matrix products  21.9 us (5%)
  local copies, waits for them, and re-layouts  13.7 us (3%)
    psum x1, blocking collectives, shards(): everyone = lax.psum((sum0 + sum1).reshape(-1), ('dp', 'seq'))  93.4 us
    all_to_all x4, waiting for transfers between devices, exchanged(): lax.all_to_all(x.reshape(devices, rows // devices, columns), ('dp', 'seq'...  88.8 us
    all_gather x1, blocking collectives, shards(): gain = lax.all_gather(norm_gain, 'dp', tiled=True).reshape(1, width)  83.3 us
    pallas_call x2, Pallas kernels, expert(): pl.pallas_call(functools.partial(expert_kernel, first), grid=(steps,), ou...  42.4 us
    all_to_all x4, starting transfers between devices, exchanged(): lax.all_to_all(x.reshape(devices, rows // devices, columns), ('dp', 'seq'...  41.5 us
    dot_general x3, matrix products, shards(): jnp.einsum('era,erb->eab', a, b, preferred_element_type=F32).astype(BF)  21.9 us
    pallas_call x2, Pallas kernels, combine(): pl.pallas_call(functools.partial(combine_kernel, last), grid=(steps,), ou...  13.4 us
    unnamed x40, local copies, waits for them, and re-layouts  13.1 us
  transfers between devices with their start and end apart: 4, of which 2 were waited for; matrix products, arithmetic and copies ran while one was open for 6% of the time, Pallas kernels for 13%

profile of v2, /device:TPU:1, one launch (start us, length us, event | category | flops | bytes accessed | tf_op | source)
XLA Modules:
  0.0 409.1 jit_solution(10541996112956314543)
XLA Ops:
  0.6 0.7 copy.40
  1.3 0.7 copy.39
  2.0 0.0 copy-start.3
  2.0 1.0 copy-done.3
  3.1 0.0 copy-start.6
  3.1 1.0 copy-done.6
  4.1 4.9 %shard_map.192 = (bf16[3072,1024]{1,0:T(8,128)(2,1)S(1)}, bf16[128,128]{1,0:T(8,128)(2,1)S(1)}) custom-call(s32[10,128]{1,0:T(8,128)S(1)} %bitcast.36, f32[10,128]{1,0:T(8,128)S(1)} %bitcast.38, bf16[128,2048]{1,0:T(8,128)(2,1)S(1)} %bitcast.40, bf16[128,2048]{1,0:T(8,128)(2,1)S(1)} %bitcast.43), custom_call_target="tpu_custom_call" | custom-call | flops 8000000000 | bytes 8000000 | tf_op jit(solution)/shard_map/pallas_call | solution.py:79
  9.0 0.0 copy-start.1
  9.0 2.6 copy-done.1
  11.7 0.0 copy-start.4
  11.7 0.0 copy-start.7
  11.7 11.9 %all-to-all-start.1 = ((bf16[128,24,1024]{2,1,0:T(8,128)(2,1)}), bf16[128,24,1024]{2,1,0:T(8,128)(2,1)}, u32[]{:S(2)}, u32[]{:S(2)}) async-start(bf16[128,24,1024]{2,1,0:T(8,128)(2,1)} %bitcast.31), calls=%async_computation.1 | async-start | bytes 12582912 | tf_op jit(solution)/shard_map/all_to_all | solution.py:286
  23.6 0.0 copy-done.4
  23.6 0.0 copy-done.7
  23.6 5.0 %shard_map.191 = (bf16[3072,1024]{1,0:T(8,128)(2,1)S(1)}, bf16[128,128]{1,0:T(8,128)(2,1)S(1)}) custom-call(s32[10,128]{1,0:T(8,128)S(1)} %bitcast.37, f32[10,128]{1,0:T(8,128)S(1)} %bitcast.39, bf16[128,2048]{1,0:T(8,128)(2,1)S(1)} %bitcast.41, bf16[128,2048]{1,0:T(8,128)(2,1)S(1)} %bitcast.44), custom_call_target="tpu_custom_call" | custom-call | flops 8000000000 | bytes 8000000 | tf_op jit(solution)/shard_map/pallas_call | solution.py:79
  28.6 0.0 copy-start
  28.6 2.7 copy-done
  31.2 68.9 %all-to-all-done.1 = bf16[128,24,1024]{2,1,0:T(8,128)(2,1)} async-done(((bf16[128,24,1024]{2,1,0:T(8,128)(2,1)}), bf16[128,24,1024]{2,1,0:T(8,128)(2,1)}, u32[]{:S(2)}, u32[]{:S(2)}) %all-to-all-start.1) | async-done | bytes 6291488 | tf_op jit(solution)/shard_map/all_to_all | solution.py:286
  100.1 0.0 copy-start.15
  100.1 9.7 %all-to-all-start = ((bf16[128,24,1024]{2,1,0:T(8,128)(2,1)}), bf16[128,24,1024]{2,1,0:T(8,128)(2,1)}, u32[]{:S(2)}, u32[]{:S(2)}) async-start(bf16[128,24,1024]{2,1,0:T(8,128)(2,1)} %bitcast.30), calls=%async_computation | async-start | bytes 12582912 | tf_op jit(solution)/shard_map/all_to_all | solution.py:286
  109.8 0.0 copy-done.15
  109.8 83.3 %all-gather = f32[16,1,128]{2,1,0:T(1,128)} all-gather(f32[1,1,128]{2,1,0:T(1,128)S(1)} %bitcast.49), channel_id=1, replica_groups=mesh['dp'=16,'seq'=8] {'dp'}, dimensions={0}, use_global_device_ids=true | all-gather | bytes 8704 | tf_op jit(solution)/shard_map/all_gather | solution.py:298
  193.1 21.2 %shard_map.193 = (bf16[3072,512]{1,0:T(8,128)(2,1)}, bf16[2,768,2048]{2,1,0:T(8,128)(2,1)}, bf16[2,768,2048]{2,1,0:T(8,128)(2,1)}, bf16[2,768,512]{2,1,0:T(8,128...) custom-call(bf16[3072,1024]{1,0:T(8,128)(2,1)} %bitcast.9.rows_ref, ...), custom_call_target="tpu_custom_call" | custom-call | flops 24999999488 | bytes 22000000 | tf_op jit(solution)/shard_map/pallas_call | solution.py:199
  214.3 0.0 all-to-all-done
  214.3 13.9 %all-to-all-start.3 = ((bf16[128,24,512]{2,1,0:T(8,128)(2,1)}), bf16[128,24,512]{2,1,0:T(8,128)(2,1)S(1)}, u32[]{:S(2)}, u32[]{:S(2)}) async-start(bf16[128,24,512]{2,1,0:T(8,128)(2,1)} %bitcast.47), calls=%async_computation.3 | async-start | bytes 6291456 | tf_op jit(solution)/shard_map/all_to_all | solution.py:286
  228.2 21.2 %shard_map.194 = (bf16[3072,512]{1,0:T(8,128)(2,1)}, bf16[2,768,2048]{2,1,0:T(8,128)(2,1)}, bf16[2,768,2048]{2,1,0:T(8,128)(2,1)}, bf16[2,768,512]{2,1,0:T(8,128...) custom-call(bf16[3072,1024]{1,0:T(8,128)(2,1)} %bitcast.5.rows_ref, ...), custom_call_target="tpu_custom_call", output_to_operand_aliasing={{1}: (7, {}), {2}: (8, {}), {3}: (9, {}), {4}: (10, {}), {5... | custom-call | flops 24999999488 | bytes 22000000 | tf_op jit(solution)/shard_map/pallas_call | solution.py:199
  249.4 0.0 copy-start.13
  249.5 0.0 copy-start.14
  249.5 19.9 %all-to-all-done.3 = bf16[128,24,512]{2,1,0:T(8,128)(2,1)S(1)} async-done(((bf16[128,24,512]{2,1,0:T(8,128)(2,1)}), bf16[128,24,512]{2,1,0:T(8,128)(2,1)S(1)}, u32[]{:S(2)}, u32[]{:S(2)}) %all-to-all-start.3) | async-done | bytes 3145760 | tf_op jit(solution)/shard_map/all_to_all | solution.py:286
  269.4 6.0 %all-to-all-start.2 = ((bf16[128,24,512]{2,1,0:T(8,128)(2,1)}), bf16[128,24,512]{2,1,0:T(8,128)(2,1)}, u32[]{:S(2)}, u32[]{:S(2)}) async-start(bf16[128,24,512]{2,1,0:T(8,128)(2,1)} %bitcast.46), calls=%async_computation.2 | async-start | bytes 6291456 | tf_op jit(solution)/shard_map/all_to_all | solution.py:286
  275.4 0.0 copy-done.13
  275.4 0.0 copy-done.14
  275.5 93.4 %psum.7 = f32[2048]{0:T(1024)S(1)} all-reduce(f32[2048]{0:T(1024)S(1)} %bitcast.48), channel_id=1, replica_groups=mesh['dp'=16,'seq'=8] {'dp','seq'}, use_global_device_ids=true, to_apply=%region_0.0 | all-reduce | flops 2048 | bytes 16384 | tf_op jit(solution)/shard_map/psum | solution.py:312
  368.8 0.6 dynamic_slice.3
  369.4 0.0 copy-start.16
  369.4 0.0 slice-start
  369.4 8.9 %convolution_convert_fusion.2 = bf16[2,2048,512]{2,1,0:T(8,128)(2,1)} fusion(bf16[2,768,2048]{2,1,0:T(8,128)(2,1)} %get-tuple-element.36, bf16[2,768,512]{2,1,0:T(8,128)(2,1)} %get-tuple-element.37), kind=kOutput, calls=%fused_computation.2 | convolution fusion | flops 3223322624 | bytes 12058624 | tf_op jit(solution)/shard_map/era,erb->eab/dot_general | solution.py:308
  378.3 0.0 copy-done.16
  378.3 0.0 slice-start.1
  378.3 6.6 %convolution_convert_fusion.1 = bf16[2,2048,512]{2,1,0:T(8,128)(2,1)} fusion(bf16[2,768,2048]{2,1,0:T(8,128)(2,1)S(1)} %copy-done.16, bf16[2,768,512]{2,1,0:T(8,128)(2,1)} %get-tuple-element.38), kind=kOutput, calls=%fused_computation.1 | convolution fusion | flops 3223322624 | bytes 12058624 | tf_op jit(solution)/shard_map/era,erb->eab/dot_general | solution.py:308
  384.9 0.0 slice-done
  384.9 0.0 slice-done.1
  384.9 0.0 copy-start.9
  384.9 0.0 copy-start.10
  384.9 6.5 %convolution_convert_fusion = bf16[2,512,2048]{2,1,0:T(8,128)(2,1)} fusion(bf16[2,768,512]{2,1,0:T(8,128)(2,1)} %get-tuple-element.39, bf16[2,768,2048]{2,1,0:T(8,128)(2,1)S(1)} %bitcast.52), kind=kOutput, calls=%fused_computation | convolution fusion | flops 3223322624 | bytes 12058624 | tf_op jit(solution)/shard_map/era,erb->eab/dot_general | solution.py:308
  391.4 0.0 copy-done.9
  391.4 0.0 copy-done.10
  391.4 0.0 copy-start.2
  391.4 4.9 %shard_map.195.refs_0_ = f32[128,2048]{1,0:T(8,128)S(1)} custom-call(bf16[128,128]{1,0:T(8,128)(2,1)S(1)} %get-tuple-element.32.tab_ref, bf16[3072,512]{1,0:T(8,128)(2,1)S(1)} %bitcast.32, f32[1,384]{1,0:T(1,128)S(1)} %copy-done.9, f32[1,384]{1,0:T(1,128)S(1)} %copy-done.10), custom_call_target="tpu_custom_call" | custom-call | flops 4000000000 | bytes 6000000 | tf_op jit(solution)/shard_map/pallas_call | solution.py:266
  396.3 0.0 copy-start.11
  396.3 1.0 copy-done.11
  397.2 0.0 all-to-all-done.2
  397.2 0.0 copy-done.2
  397.2 0.0 copy-start.5
  397.2 1.0 copy-done.5
  398.3 0.0 copy-start.8
  398.3 1.0 copy-done.8
  399.3 0.0 copy-start.12
  399.3 1.2 copy-done.12
  400.6 8.6 %shard_map.196 = bf16[128,2048]{1,0:T(8,128)(2,1)} custom-call(bf16[128,128]{1,0:T(8,128)(2,1)S(1)} %get-tuple-element.23.tab_ref, bf16[3072,512]{1,0:T(8,128)(2,1)} %bitcast.11.rows_ref, f32[1,384]{1,0:T(1,128)S(1)} %copy-done.9, f32[1,384]{1,0:T(1,128)S(1)} %copy-done.10, f32[128,2048]{1,0:T(8,128)S(1)} %copy-done.12, bf16[128,2048]{1,0:T(8,128)(2,1)S(1)} %bitcast.42, ...), custom_call_target="tpu_custom_call" | custom-call | flops 4000000000 | bytes 6000000 | tf_op jit(solution)/shard_map/pallas_call | solution.py:266
  (2 shorter events, 0.0 us)
Async XLA Ops:
  2.0 1.0 copy-start.3
  3.1 1.0 copy-start.6
  9.0 2.6 copy-start.1
  11.7 11.9 %copy-start.4 = (bf16[1,128,2048]{2,1,0:T(8,128)(2,1)S(1)}, bf16[1,128,2048]{2,1,0:T(8,128)(2,1)}, u32[]{:S(2)}) copy-start(bf16[1,128,2048]{2,1,0:T(8,128)(2,1)} %param.16) | copy-start | bytes 1572868
  11.7 11.9 %copy-start.7 = (bf16[1,128,2048]{2,1,0:T(8,128)(2,1)S(1)}, bf16[1,128,2048]{2,1,0:T(8,128)(2,1)}, u32[]{:S(2)}) copy-start(bf16[1,128,2048]{2,1,0:T(8,128)(2,1)} %param.17) | copy-start | bytes 1572868
  11.7 88.4 %all-to-all-start.1 = ((bf16[128,24,1024]{2,1,0:T(8,128)(2,1)}), bf16[128,24,1024]{2,1,0:T(8,128)(2,1)}, u32[]{:S(2)}, u32[]{:S(2)}) async-start(bf16[128,24,1024]{2,1,0:T(8,128)(2,1)} %bitcast.31), calls=%async_computation.1 | async-start | bytes 12582912 | tf_op jit(solution)/shard_map/all_to_all | solution.py:286
  28.6 2.7 copy-start
  100.1 9.7 %copy-start.15 = (f32[128]{0:T(128)S(1)}, f32[128]{0:T(128)}, u32[]{:S(2)}) copy-start(f32[128]{0:T(128)} %param.18) | copy-start | bytes 1540
  100.1 114.2 %all-to-all-start = ((bf16[128,24,1024]{2,1,0:T(8,128)(2,1)}), bf16[128,24,1024]{2,1,0:T(8,128)(2,1)}, u32[]{:S(2)}, u32[]{:S(2)}) async-start(bf16[128,24,1024]{2,1,0:T(8,128)(2,1)} %bitcast.30), calls=%async_computation | async-start | bytes 12582912 | tf_op jit(solution)/shard_map/all_to_all | solution.py:286
  214.3 55.0 %all-to-all-start.3 = ((bf16[128,24,512]{2,1,0:T(8,128)(2,1)}), bf16[128,24,512]{2,1,0:T(8,128)(2,1)S(1)}, u32[]{:S(2)}, u32[]{:S(2)}) async-start(bf16[128,24,512]{2,1,0:T(8,128)(2,1)} %bitcast.47), calls=%async_computation.3 | async-start | bytes 6291456 | tf_op jit(solution)/shard_map/all_to_all | solution.py:286
  249.4 26.0 %copy-start.13 = (f32[1,2048]{1,0:T(1,128)S(1)}, f32[1,2048]{1,0:T(1,128)}, u32[]{:S(2)}) copy-start(f32[1,2048]{1,0:T(1,128)} %get-tuple-element.34) | copy-start | bytes 24580
  249.5 26.0 %copy-start.14 = (f32[1,2048]{1,0:T(1,128)S(1)}, f32[1,2048]{1,0:T(1,128)}, u32[]{:S(2)}) copy-start(f32[1,2048]{1,0:T(1,128)} %get-tuple-element.35) | copy-start | bytes 24580
  269.4 127.9 %all-to-all-start.2 = ((bf16[128,24,512]{2,1,0:T(8,128)(2,1)}), bf16[128,24,512]{2,1,0:T(8,128)(2,1)}, u32[]{:S(2)}, u32[]{:S(2)}) async-start(bf16[128,24,512]{2,1,0:T(8,128)(2,1)} %bitcast.46), calls=%async_computation.2 | async-start | bytes 6291456 | tf_op jit(solution)/shard_map/all_to_all | solution.py:286
  369.4 8.9 %copy-start.16 = (bf16[2,768,2048]{2,1,0:T(8,128)(2,1)S(1)}, bf16[2,768,2048]{2,1,0:T(8,128)(2,1)}, u32[]{:S(2)}) copy-start(bf16[2,768,2048]{2,1,0:T(8,128)(2,1)} %get-tuple-element.36) | copy-start | bytes 18874372
  369.4 15.5 %slice-start = ((s8[6291456]{0:T(1024)(128)(4,1)}), s8[4194304]{0:T(1024)(128)(4,1)S(1)}, s32[]{:S(2)}) async-start(s8[6291456]{0:T(1024)(128)(4,1)} %bitcast.51), calls=%async_computation.4 | async-start | bytes 8388608
  378.3 6.6 %slice-start.1 = ((s8[6291456]{0:T(1024)(128)(4,1)}), s8[2097152]{0:T(1024)(128)(4,1)S(1)}, s32[]{:S(2)}) async-start(s8[6291456]{0:T(1024)(128)(4,1)} %bitcast.51), calls=%async_computation.5 | async-start | bytes 4194304
  384.9 6.5 %copy-start.9 = (f32[1,384]{1,0:T(1,128)S(1)}, f32[1,384]{1,0:T(1,128)}, u32[]{:S(2)}) copy-start(f32[1,384]{1,0:T(1,128)} %constant.22.clone.slot_ref) | copy-start | bytes 4612
  384.9 6.5 %copy-start.10 = (f32[1,384]{1,0:T(1,128)S(1)}, f32[1,384]{1,0:T(1,128)}, u32[]{:S(2)}) copy-start(f32[1,384]{1,0:T(1,128)} %constant.23.clone.part_ref) | copy-start | bytes 4612
  391.4 5.8 %copy-start.2 = (f32[16,1,128]{2,1,0:T(1,128)S(1)}, f32[16,1,128]{2,1,0:T(1,128)}, u32[]{:S(2)}) copy-start(f32[16,1,128]{2,1,0:T(1,128)} %all-gather) | copy-start | bytes 24580
  396.3 1.0 copy-start.11
  397.2 1.0 copy-start.5
  398.3 1.0 copy-start.8
  399.3 1.2 copy-start.12

commit v3 on v2

v3 whole, which is shorter than its diff:
```python
import jax
import jax.numpy as jnp
import numpy as np
from jax import lax
from jax.experimental import pallas as pl
from jax.experimental.pallas import tpu as pltpu
from jax.sharding import PartitionSpec as P

TOP = 10
EPSILON = 1e-06
CAP = 6
BF = jnp.bfloat16
F32 = jnp.float32
VMEM_LIMIT = 62 * 2**20
MESH = pl.DeviceIdType.MESH
STRIDE = 37


def dot(a, b, ca=1, cb=0):
    return lax.dot_general(a, b, (((ca,), (cb,)), ((), ())), preferred_element_type=F32)


def dispatch_kernel(ids_ref, w_ref, dest_ref, hid_ref, cot_ref, send_ref, tab_ref, tab_s, wt_s, src_s):
    which, step = pl.program_id(0), pl.program_id(1)
    tokens = hid_ref.shape[0]
    half = hid_ref.shape[1] // 2
    devices = tab_s.shape[0]

    @pl.when((which == 0) & (step == 0))
    def _():
        for h in range(2):
            src_s[h * 2 * tokens : h * 2 * tokens + tokens, :] = hid_ref[:, h * half : (h + 1) * half]
            src_s[h * 2 * tokens + tokens : (h + 1) * 2 * tokens, :] = cot_ref[:, h * half : (h + 1) * half]

    @pl.when(step == 0)
    def _():
        expert = jnp.broadcast_to(2 * dest_ref[...] + which, (devices, tokens))
        hit = jnp.zeros((devices, tokens), F32)
        weight = jnp.zeros((devices, tokens), F32)
        for k in range(TOP):
            same = ids_ref[k : k + 1, :] == expert
            hit = hit + jnp.where(same, 1.0, 0.0)
            weight = weight + jnp.where(same, w_ref[k : k + 1, :], 0.0)
        earlier = lax.broadcasted_iota(jnp.int32, (tokens, tokens), 0) < lax.broadcasted_iota(
            jnp.int32, (tokens, tokens), 1
        )
        rank = dot(hit.astype(BF), jnp.where(earlier, 1.0, 0.0).astype(BF))
        table = jnp.where(hit > 0.0, rank, -1.0)
        tab_s[...] = table
        tab_ref[0] = table.astype(BF)
        wt_s[...] = weight

    group = send_ref.shape[1] // 24
    at = pl.ds(pl.multiple_of(step * group, group), group)
    shape = (group, 24, tokens)
    table = jnp.broadcast_to(tab_s[at, :][:, None, :], shape)
    weight = jnp.broadcast_to(wt_s[at, :][:, None, :], shape)
    row = lax.broadcasted_iota(jnp.int32, shape, 1)
    in_half = jnp.where(row >= 12, 1, 0)
    row = row - 12 * in_half
    is_grad = jnp.where(row >= CAP, 1, 0)
    slot = (row - CAP * is_grad).astype(F32)
    flat = (group * 24, tokens)
    pick = jnp.where(table == slot, 1.0, 0.0)
    scale = jnp.sum(
        jnp.where(is_grad == 1, pick * weight, jnp.where(lax.broadcasted_iota(jnp.int32, shape, 2) == 0, 1.0, 0.0)),
        axis=2,
        keepdims=True,
    ).reshape(flat[0], 1)
    kind = 2 * in_half + is_grad
    pieces = [jnp.where(kind == m, pick, 0.0).reshape(flat).astype(BF) for m in range(4)]
    left = jnp.concatenate(pieces, axis=1)
    send_ref[0] = (dot(left, src_s[...]) * scale).astype(BF)


def dispatch(devices, ids_t, w_t, dest, hidden, cot):
    tokens, width = hidden.shape
    steps = 8
    rows = devices * 24
    whole = lambda *s: pl.BlockSpec(s, lambda i, g: tuple(0 for _ in s))
    return pl.pallas_call(
        dispatch_kernel,
        grid=(2, steps),
        out_shape=[
            jax.ShapeDtypeStruct((2, rows, width // 2), BF),
            jax.ShapeDtypeStruct((2, devices, tokens), BF),
        ],
        in_specs=[
            whole(TOP, tokens),
            whole(TOP, tokens),
            whole(devices, 1),
            whole(tokens, width),
            whole(tokens, width),
        ],
        out_specs=[
            pl.BlockSpec((1, rows // steps, width // 2), lambda i, g: (i, g, 0)),
            pl.BlockSpec((1, devices, tokens), lambda i, g: (i, 0, 0)),
        ],
        scratch_shapes=[
            pltpu.VMEM((devices, tokens), F32),
            pltpu.VMEM((devices, tokens), F32),
            pltpu.VMEM((4 * tokens, width // 2), BF),
        ],
        compiler_params=pltpu.CompilerParams(vmem_limit_bytes=32 * 2**20),
        cost_estimate=pl.CostEstimate(flops=8 * 10**9, bytes_accessed=16 * 10**6, transcendentals=0),
        name="dispatch",
    )(ids_t, w_t, dest, hidden, cot)


def order_in():
    m = np.zeros((192, 192), np.float32)
    for s in range(8):
        for h in range(2):
            for a in range(2):
                for r in range(CAP):
                    m[a * 96 + h * 48 + s * CAP + r, s * 24 + h * 12 + a * CAP + r] = 1
    return m


def order_out():
    m = np.zeros((192, 192), np.float32)
    for s in range(8):
        for q in range(4):
            for r in range(CAP):
                m[s * 24 + q * CAP + r, q * 48 + s * CAP + r] = 1
    return m


def place(n):
    v = ((n + 1) * STRIDE) % 128
    return v // 32, (v // 8) % 4, (v // 2) % 4, v % 2


def here():
    dp, seq = lax.axis_index("dp"), lax.axis_index("seq")
    return dp % 4, dp // 4, seq // 2, seq % 2


def device_at(n, sign):
    x, y, z, core = here()
    dx, dy, dz, dcore = place(n)
    x, y, z = (x + sign * dx + 4) % 4, (y + sign * dy + 4) % 4, (z + sign * dz + 4) % 4
    return y * 4 + x, z * 2 + (core + dcore) % 2


def core_kernel(
    send, gain_in, gate, up, down, into_ref, out_of_ref,
    back, ret, came, total_ref, gain_ref, d_gate, d_up, d_down,
    gain_s, g_gate, g_up, g_down, raw_s, rows_s, norm_s, grad_s, act_s, gb_s, ub_s, ret_s, dw_s, dd_s,
    sum_s, piece_s, arrive_s, share_s, share_in_s,
    w_sem, gain_send, gain_recv, f_send, f_recv, r_send, r_recv, load_sem, store_sem, dw_sem, t_send, t_recv,
):
    dp, seq = lax.axis_index("dp"), lax.axis_index("seq")
    devices = 128
    width = norm_s.shape[2]
    half, quarter = width // 2, width // 4
    group = 32
    rows = group * CAP

    def gain_copy(i):
        return pltpu.make_async_remote_copy(
            gain_in, gain_s.at[dp], gain_send, gain_recv, device_id=((dp + i) % 16, seq), device_id_type=MESH
        )

    own_gain = pltpu.make_async_copy(gain_in, gain_s.at[dp], gain_recv)
    own_gain.start()

    @pl.loop(1, 16)
    def _(i):
        gain_copy(i).start()

    def at(n, size=1):
        return pl.ds(pl.multiple_of(n * 24, 8), size * 24)

    for w in range(2):
        @pl.loop(0, devices - 1)
        def _(n):
            pltpu.make_async_remote_copy(
                send.at[w, at(n)],
                came.at[w, at(n)],
                f_send.at[w],
                f_recv.at[w * 4 + n // group],
                device_id=device_at(n, 1),
                device_id_type=MESH,
            ).start()

        pltpu.make_async_copy(send.at[w, at(devices - 1)], came.at[w, at(devices - 1)], f_recv.at[w * 4 + 3]).start()

    loads = [
        pltpu.make_async_copy(gate, g_gate, w_sem.at[0]),
        pltpu.make_async_copy(up, g_up, w_sem.at[1]),
        pltpu.make_async_copy(down, g_down, w_sem.at[2]),
    ]
    for c in loads:
        c.start()
    for c in loads:
        c.wait()
    pltpu.make_async_copy(gain_s, gain_s, gain_recv).wait()
    gain_ref[...] = jnp.concatenate([gain_s[i] for i in range(16)], axis=1)
    sum_s[...] = jnp.zeros_like(sum_s)

    @pl.loop(0, 8)
    def _(step):
        w, g = step // 4, step % 4
        slab = at(g * group, group)
        pltpu.make_async_copy(came.at[w, slab], came.at[w, slab], f_recv.at[step]).wait()
        load = pltpu.make_async_copy(came.at[w, slab], rows_s, load_sem)
        load.start()
        load.wait()
        mine = pl.ds(pl.multiple_of(g * rows, rows), rows)
        for b in range(4):
            moved = dot(into_ref[...], rows_s[b * 192 : (b + 1) * 192, :])
            there = pl.ds(pl.multiple_of(g * rows + b * 48, 16), 48)
            for h in range(2):
                raw_s[b * 48 : (b + 1) * 48, h * half : (h + 1) * half] = moved[h * 48 : (h + 1) * 48, :]
                grad_s[w, there, h * half : (h + 1) * half] = moved[96 + h * 48 : 96 + (h + 1) * 48, :].astype(BF)
        raw = raw_s[...]
        root = lax.rsqrt(jnp.mean(raw * raw, axis=1, keepdims=True) + EPSILON)
        normed = (raw * root * gain_ref[...]).astype(BF)
        norm_s[w, mine, :] = normed
        pre_gate = dot(normed, g_gate[w])
        pre_up = dot(normed, g_up[w])
        sig = jax.nn.sigmoid(pre_gate)
        silu = pre_gate * sig
        act_s[w, mine, :] = (silu * pre_up).astype(BF)
        grad_act = dot(grad_s[w, mine, :], g_down[w], 1, 1)
        gate_back = (grad_act * pre_up * sig * (1.0 + pre_gate * (1.0 - sig))).astype(BF)
        up_back = (grad_act * silu).astype(BF)
        gb_s[w, mine, :] = gate_back
        ub_s[w, mine, :] = up_back
        returned = (dot(gate_back, g_gate[w], 1, 1) + dot(up_back, g_up[w], 1, 1)).astype(BF)
        sum_s[...] += jnp.sum(returned.astype(F32) * (raw_s[...] * root), axis=0, keepdims=True)
        for b in range(4):
            part = returned[b * 48 : (b + 1) * 48, :]
            stacked = jnp.concatenate([part[:, q * quarter : (q + 1) * quarter] for q in range(4)], axis=0)
            ret_s[b * 192 : (b + 1) * 192, :] = dot(out_of_ref[...], stacked).astype(BF)
        store = pltpu.make_async_copy(ret_s, ret.at[w, slab], store_sem)
        store.start()
        store.wait()

        @pl.loop(g * group, jnp.minimum(g * group + group, devices - 1))
        def _(n):
            pltpu.make_async_remote_copy(
                ret.at[w, at(n)],
                back.at[w, at(n)],
                r_send,
                r_recv.at[w],
                device_id=device_at(n, -1),
                device_id_type=MESH,
            ).start()

    for w in range(2):
        last = at(devices - 1)
        pltpu.make_async_copy(ret.at[w, last], back.at[w, last], r_recv.at[w]).start()

    for p in range(16):
        piece_s[p] = sum_s[:, p * 128 : (p + 1) * 128]

    def piece(i):
        return pltpu.make_async_remote_copy(
            piece_s.at[(dp + i) % 16], arrive_s.at[i], t_send.at[0], t_recv.at[0],
            device_id=((dp + i) % 16, seq), device_id_type=MESH,
        )

    @pl.loop(1, 16)
    def _(i):
        piece(i).start()

    block = 256
    for w in range(2):
        if w == 1:
            for c in stores:
                c.wait()

        @pl.loop(0, width // block)
        def _(j):
            lanes = pl.ds(pl.multiple_of(j * block, block), block)
            left = norm_s[w, :, lanes]
            dw_s[0, lanes, :] = dot(left, gb_s[w], 0, 0).astype(BF)
            dw_s[1, lanes, :] = dot(left, ub_s[w], 0, 0).astype(BF)
            dd_s[:, lanes] = dot(act_s[w], grad_s[w, :, lanes], 0, 0).astype(BF)

        stores = [
            pltpu.make_async_copy(dw_s.at[0], d_gate.at[w], dw_sem.at[0]),
            pltpu.make_async_copy(dw_s.at[1], d_up.at[w], dw_sem.at[1]),
            pltpu.make_async_copy(dd_s, d_down.at[w], dw_sem.at[2]),
        ]
        for c in stores:
            c.start()

    fifteen = arrive_s.at[pl.ds(1, 15)]
    pltpu.make_async_copy(fifteen, fifteen, t_recv.at[0]).wait()
    share = piece_s[dp]
    for i in range(1, 16):
        share = share + arrive_s[i]
    share_s[...] = share

    def to_copy(i):
        return pltpu.make_async_remote_copy(
            share_s, share_in_s.at[i], t_send.at[1], t_recv.at[1], device_id=(dp, (seq + i) % 8), device_id_type=MESH
        )

    @pl.loop(1, 8)
    def _(i):
        to_copy(i).start()

    for c in stores:
        c.wait()
    for w in range(2):
        pltpu.make_async_copy(back.at[w], back.at[w], r_recv.at[w]).wait()
    seven = share_in_s.at[pl.ds(1, 7)]
    pltpu.make_async_copy(seven, seven, t_recv.at[1]).wait()
    for i in range(1, 8):
        share = share + share_in_s[i]
    total_ref[...] = share

    most = at(0, devices - 1)
    for w in range(2):
        pltpu.make_async_copy(send.at[w, most], send.at[w, most], f_send.at[w]).wait()
        pltpu.make_async_copy(ret.at[w, most], ret.at[w, most], r_send).wait()
    pltpu.make_async_copy(fifteen, fifteen, t_send.at[0]).wait()
    pltpu.make_async_copy(seven, seven, t_send.at[1]).wait()
    pltpu.make_async_copy(gain_s.at[pl.ds(1, 15)], gain_s.at[pl.ds(1, 15)], gain_send).wait()


def core(send, gain, gate, up, down):
    _, total, half = send.shape
    width = 2 * half
    experts, _, hidden = gate.shape
    slots = total // 4
    hbm = pl.BlockSpec(memory_space=pl.ANY)
    vmem = pl.BlockSpec(memory_space=pltpu.VMEM)
    back = jax.ShapeDtypeStruct((2, total, width // 4), BF)
    dma = pltpu.SemaphoreType.DMA
    outs = pl.pallas_call(
        core_kernel,
        out_shape=[
            back,
            back,
            jax.ShapeDtypeStruct(send.shape, BF),
            jax.ShapeDtypeStruct((1, 128), F32),
            jax.ShapeDtypeStruct((1, width), F32),
            jax.ShapeDtypeStruct(gate.shape, BF),
            jax.ShapeDtypeStruct(up.shape, BF),
            jax.ShapeDtypeStruct(down.shape, BF),
        ],
        in_specs=[hbm] * 5 + [vmem] * 2,
        out_specs=[hbm] * 3 + [vmem] * 2 + [hbm] * 3,
        scratch_shapes=[
            pltpu.VMEM((16, 1, 128), F32),
            pltpu.VMEM(gate.shape, BF),
            pltpu.VMEM(up.shape, BF),
            pltpu.VMEM(down.shape, BF),
            pltpu.VMEM((slots // 4, width), F32),
            pltpu.VMEM((total // 4, half), BF),
            pltpu.VMEM((experts, slots, width), BF),
            pltpu.VMEM((experts, slots, width), BF),
            pltpu.VMEM((experts, slots, hidden), BF),
            pltpu.VMEM((experts, slots, hidden), BF),
            pltpu.VMEM((experts, slots, hidden), BF),
            pltpu.VMEM((total // 4, width // 4), BF),
            pltpu.VMEM((2, width, hidden), BF),
            pltpu.VMEM((hidden, width), BF),
            pltpu.VMEM((1, width), F32),
            pltpu.VMEM((16, 1, 128), F32),
            pltpu.VMEM((16, 1, 128), F32),
            pltpu.VMEM((1, 128), F32),
            pltpu.VMEM((8, 1, 128), F32),
            dma((3,)), dma, dma, dma((2,)), dma((8,)), dma, dma((2,)), dma, dma, dma((3,)), dma((2,)), dma((2,)),
        ],
        compiler_params=pltpu.CompilerParams(has_side_effects=True, vmem_limit_bytes=VMEM_LIMIT),
        cost_estimate=pl.CostEstimate(flops=40 * 10**9, bytes_accessed=80 * 10**6, transcendentals=10**6),
        name="core",
    )(send, gain, gate, up, down, jnp.asarray(order_in(), BF), jnp.asarray(order_out(), BF))
    return outs[0], outs[3], outs[4], outs[5], outs[6], outs[7]


def combine_kernel(tab_ref, rows_ref, slot_ref, part_ref, hid_ref, cot_ref, gain_ref, out_ref, acc):
    step = pl.program_id(0) * pl.num_programs(1) + pl.program_id(1)
    count = rows_ref.shape[1]
    group, tokens = tab_ref.shape[1:]

    @pl.when(step == 0)
    def _():
        acc[...] = jnp.zeros_like(acc)

    at = lax.broadcasted_iota(jnp.int32, (group, count), 1) - 24 * lax.broadcasted_iota(
        jnp.int32, (group, count), 0
    )
    spread = jnp.where((at >= 0) & (at < 24), 1.0, 0.0).astype(BF)
    table = dot(tab_ref[0], spread, 0, 0)
    pick = jnp.where(table == slot_ref[...], 1.0, 0.0)
    left = jnp.concatenate(
        [jnp.where(part_ref[...] == float(q), pick, 0.0).astype(BF) for q in range(4)], axis=0
    )
    acc[...] += dot(left, rows_ref[0])

    @pl.when(step == pl.num_programs(0) * pl.num_programs(1) - 1)
    def _():
        summed = jnp.concatenate([acc[q * tokens : (q + 1) * tokens, :] for q in range(4)], axis=1)
        raw = hid_ref[...].astype(F32)
        root = lax.rsqrt(jnp.mean(raw * raw, axis=1, keepdims=True) + EPSILON)
        scaled = raw * root
        gained = summed * gain_ref[...]
        centre = jnp.mean(gained * scaled, axis=1, keepdims=True)
        out_ref[...] = (cot_ref[...].astype(F32) + root * (gained - scaled * centre)).astype(BF)


def combine(table, back, tokens, hidden, cot, gain):
    _, total, quarter = back.shape
    width = 4 * quarter
    devices = table.shape[1]
    steps = 8
    group = devices // steps
    place_in = np.arange(group * 24) % 24
    slot = jnp.asarray((place_in % CAP)[None, :], F32)
    part = jnp.asarray((place_in // CAP)[None, :], F32)
    whole = lambda *s: pl.BlockSpec(s, lambda i, g: tuple(0 for _ in s))
    return pl.pallas_call(
        combine_kernel,
        grid=(2, steps),
        out_shape=jax.ShapeDtypeStruct((tokens, width), BF),
        in_specs=[
            pl.BlockSpec((1, group, tokens), lambda i, g: (i, g, 0)),
            pl.BlockSpec((1, group * 24, quarter), lambda i, g: (i, g, 0)),
            whole(1, group * 24),
            whole(1, group * 24),
            whole(tokens, width),
            whole(tokens, width),
            whole(1, width),
        ],
        out_specs=whole(tokens, width),
        scratch_shapes=[pltpu.VMEM((4 * tokens, quarter), F32)],
        compiler_params=pltpu.CompilerParams(vmem_limit_bytes=32 * 2**20),
        cost_estimate=pl.CostEstimate(flops=8 * 10**9, bytes_accessed=10 * 10**6, transcendentals=0),
        name="combine",
    )(table, back, slot, part, hidden, cot, gain)


def shards(
    hidden_in, cotangent, norm_gain, route_weights, expert_ids, expert_gate, expert_up, expert_down
):
    hidden, cot = hidden_in[0], cotangent[0]
    tokens, width = hidden.shape
    devices = lax.axis_size("dp") * lax.axis_size("seq")
    ids_t = expert_ids[0].T
    w_t = route_weights[0].T
    dp, seq = device_at(jnp.arange(devices, dtype=jnp.int32), 1)
    dest = (dp * 8 + seq).astype(jnp.int32).reshape(devices, 1)
    send, table = dispatch(devices, ids_t, w_t, dest, hidden, cot)
    back, grad_gain, gain, grad_gate, grad_up, grad_down = core(
        send, norm_gain.reshape(1, -1), expert_gate, expert_up, expert_down
    )
    grad_hidden = combine(table, back, tokens, hidden, cot, gain)
    return grad_hidden[None], grad_gain.reshape(-1), grad_gate, grad_up, grad_down


def solution(mesh):
    rows = P("dp", "seq", None)
    experts = P(("dp", "seq"), None, None)
    return jax.shard_map(
        shards,
        mesh=mesh,
        in_specs=(rows, rows, P("dp"), rows, rows, experts, experts, experts),
        out_specs=(rows, P("dp"), experts, experts, experts),
        check_vma=False,
    )
```

time: 410 us -> 273 us (0.67)
  Pallas kernels: 65.7 us -> 250 us
  blocking collectives: 177 us -> 0 us
  waiting for transfers between devices: 88.8 us -> 0 us
  starting transfers between devices: 41.5 us -> 0 us
  matrix products: 21.9 us -> 0 us
  local copies, waits for them, and re-layouts: 13.7 us -> 21.4 us
    pallas_call x6 -> x3, Pallas kernels: 65.7 us -> 250 us  [the longest x1 229 us: core(): pl.pallas_call(core_kernel, out_shape=[back, back, jax.ShapeDtypeStruct(s...]
    psum x1 -> x0, blocking collectives: 93.4 us -> none  [shards(): everyone = lax.psum((sum0 + sum1).reshape(-1), ('dp', 'seq'))]
    all_to_all x4 -> x0, waiting for transfers between devices: 88.8 us -> none  [exchanged(): lax.all_to_all(x.reshape(devices, rows // devices, columns), ('dp', 'seq'...]
    all_gather x1 -> x0, blocking collectives: 83.3 us -> none  [shards(): gain = lax.all_gather(norm_gain, 'dp', tiled=True).reshape(1, width)]
    all_to_all x4 -> x0, starting transfers between devices: 41.5 us -> none  [exchanged(): lax.all_to_all(x.reshape(devices, rows // devices, columns), ('dp', 'seq'...]
    dot_general x3 -> x0, matrix products: 21.9 us -> none  [shards(): jnp.einsum('era,erb->eab', a, b, preferred_element_type=F32).astype(BF)]
    unnamed x40 -> x32, local copies, waits for them, and re-layouts: 13.1 us -> 21.4 us
  transfers between devices with their start and end apart: 4 -> 0, of which waited for: 2 -> 0; matrix products, arithmetic and copies ran while one was open for 6% -> 0% of each run, Pallas kernels for 13% -> 0%
where the time goes in v3:
time: 273 us; the launch traced here: 272 us
  Pallas kernels  250 us (92%)
  local copies, waits for them, and re-layouts  21.4 us (8%)
    pallas_call x1, Pallas kernels, core(): pl.pallas_call(core_kernel, out_shape=[back, back, jax.ShapeDtypeStruct(s...  229 us
    unnamed x32, local copies, waits for them, and re-layouts  21.4 us
    pallas_call x1, Pallas kernels, combine(): pl.pallas_call(combine_kernel, grid=(2, steps), out_shape=jax.ShapeDtypeS...  10.9 us
    pallas_call x1, Pallas kernels, dispatch(): pl.pallas_call(dispatch_kernel, grid=(2, steps), out_shape=[jax.ShapeDtyp...  10.2 us

profile of v3, /device:TPU:1, one launch (start us, length us, event | category | flops | bytes accessed | tf_op | source)
XLA Modules:
  0.0 272.2 jit_solution(9594731666270825955)
XLA Ops:
  0.7 0.7 copy.21
  1.4 0.7 copy.22
  2.1 0.3 fusion.9.dest_ref
  2.4 0.0 copy-start
  2.4 1.0 copy-done
  3.4 0.0 copy-start.2
  3.4 1.0 copy-done.2
  4.5 10.2 %dispatch.1 = (bf16[2,3072,1024]{2,1,0:T(8,128)(2,1)S(1)}, bf16[2,128,128]{2,1,0:T(8,128)(2,1)S(1)}) custom-call(s32[10,128]{1,0:T(8,128)S(1)} %bitcast.16, f32[10,128]{1,0:T(8,128)S(1)} %bitcast.15, s32[128,1]{1,0:T(8,128)S(1)} %fusion.9.dest_ref, bf16[128,2048]{1,0:T(8,128)(2,1)S(1)} %bitcast.17, bf16[128,2048]{1,0:T(8,128)(2,1)S(1)} %bitcast.19), custom_call_target="tpu_custom_call" | custom-call | flops 8000000000 | bytes 16000000 | tf_op jit(solution)/shard_map/dispatch/pallas_call | solution.py:81
  14.7 0.0 copy-start.6
  14.7 4.5 %copy-done.6 = bf16[2,3072,1024]{2,1,0:T(8,128)(2,1)} copy-done((bf16[2,3072,1024]{2,1,0:T(8,128)(2,1)}, bf16[2,3072,1024]{2,1,0:T(8,128)(2,1)S(1)}, u32[]{:S(2)}) %copy-start.6) | copy-done | bytes 12582936
  19.2 0.0 copy-start.1
  19.2 0.0 copy-start.3
  19.2 0.0 copy-start.4
  19.2 0.0 copy-start.5
  19.2 228.6 %core.1 = (bf16[2,3072,512]{2,1,0:T(8,128)(2,1)}, bf16[2,3072,512]{2,1,0:T(8,128)(2,1)}, bf16[2,3072,1024]{2,1,0:T(8,128)(2,1)}, f32[1,128]{1,0:T(1,128)}, f32[1...) custom-call(bf16[2,3072,1024]{2,1,0:T(8,128)(2,1)} %copy-done.6, ...), custom_call_target="tpu_custom_call" | custom-call | flops 40000000000 | bytes 80000000 | tf_op jit(solution)/shard_map/core/pallas_call | solution.py:335
  247.9 0.0 copy-done.1
  247.9 0.0 copy-done.3
  247.9 0.0 copy-done.4
  247.9 0.0 copy-done.5
  247.9 0.0 copy-start.7
  247.9 2.8 %copy-done.7 = bf16[2,3072,512]{2,1,0:T(8,128)(2,1)S(1)} copy-done((bf16[2,3072,512]{2,1,0:T(8,128)(2,1)S(1)}, bf16[2,3072,512]{2,1,0:T(8,128)(2,1)}, u32[]{:S(2)}) %copy-start.7) | copy-done | bytes 6291480
  250.7 0.0 copy-start.8
  250.7 0.7 copy-done.8
  251.4 0.0 copy-start.12
  251.4 0.0 copy-start.11
  251.4 10.9 %combine.1 = bf16[128,2048]{1,0:T(8,128)(2,1)} custom-call(bf16[2,128,128]{2,1,0:T(8,128)(2,1)S(1)} %get-tuple-element.13.tab_ref, bf16[2,3072,512]{2,1,0:T(8,128)(2,1)S(1)} %copy-done.7, f32[1,384]{1,0:T(1,128)S(1)} %copy-done.5, f32[1,384]{1,0:T(1,128)S(1)} %copy-done.4, bf16[128,2048]{1,0:T(8,128)(2,1)S(1)} %bitcast.18, bf16[128,2048]{1,0:T(8,128)(2,1)S(1)} %bitcast.20, ...), custom_call_target="tpu_custom_call" | custom-call | flops 8000000000 | bytes 10000000 | tf_op jit(solution)/shard_map/combine/pallas_call | solution.py:419
  262.3 0.0 copy-done.12
  262.3 0.5 copy.27
  262.8 0.0 copy-done.11
  262.8 0.0 copy-start.10
  262.8 2.1 copy.28
  264.9 1.6 copy-done.10
  266.5 0.0 copy-start.9
  266.5 2.1 copy.29
  268.6 1.6 copy-done.9
  270.2 2.0 copy.30
Async XLA Ops:
  2.4 1.0 copy-start
  3.4 1.0 copy-start.2
  14.7 4.5 %copy-start.6 = (bf16[2,3072,1024]{2,1,0:T(8,128)(2,1)}, bf16[2,3072,1024]{2,1,0:T(8,128)(2,1)S(1)}, u32[]{:S(2)}) copy-start(bf16[2,3072,1024]{2,1,0:T(8,128)(2,1)S(1)} %get-tuple-element.14.send) | copy-start | bytes 37748740
  19.2 228.7 %copy-start.1 = (bf16[1,128,2048]{2,1,0:T(8,128)(2,1)S(1)}, bf16[1,128,2048]{2,1,0:T(8,128)(2,1)}, u32[]{:S(2)}) copy-start(bf16[1,128,2048]{2,1,0:T(8,128)(2,1)} %param.12) | copy-start | bytes 1572868
  19.2 228.7 %copy-start.3 = (bf16[1,128,2048]{2,1,0:T(8,128)(2,1)S(1)}, bf16[1,128,2048]{2,1,0:T(8,128)(2,1)}, u32[]{:S(2)}) copy-start(bf16[1,128,2048]{2,1,0:T(8,128)(2,1)} %param.13) | copy-start | bytes 1572868
  19.2 228.7 %copy-start.4 = (f32[1,384]{1,0:T(1,128)S(1)}, f32[1,384]{1,0:T(1,128)}, u32[]{:S(2)}) copy-start(f32[1,384]{1,0:T(1,128)} %constant.148.clone.part_ref) | copy-start | bytes 4612
  19.2 228.7 %copy-start.5 = (f32[1,384]{1,0:T(1,128)S(1)}, f32[1,384]{1,0:T(1,128)}, u32[]{:S(2)}) copy-start(f32[1,384]{1,0:T(1,128)} %constant.147.clone.slot_ref) | copy-start | bytes 4612
  247.9 2.8 %copy-start.7 = (bf16[2,3072,512]{2,1,0:T(8,128)(2,1)S(1)}, bf16[2,3072,512]{2,1,0:T(8,128)(2,1)}, u32[]{:S(2)}) copy-start(bf16[2,3072,512]{2,1,0:T(8,128)(2,1)} %get-tuple-element.15.rows_ref) | copy-start | bytes 18874372
  250.7 0.7 copy-start.8
  251.4 10.9 %copy-start.12 = (f32[1,128]{1,0:T(1,128)S(1)}, f32[1,128]{1,0:T(1,128)}, u32[]{:S(2)}) copy-start(f32[1,128]{1,0:T(1,128)} %get-tuple-element.17) | copy-start | bytes 1540
  251.4 11.4 %copy-start.11 = (bf16[2,2048,512]{2,1,0:T(8,128)(2,1)S(1)}, bf16[2,2048,512]{2,1,0:T(8,128)(2,1)}, u32[]{:S(2)}) copy-start(bf16[2,2048,512]{2,1,0:T(8,128)(2,1)} %get-tuple-element.28) | copy-start | bytes 12582916
  262.8 3.7 %copy-start.10 = (bf16[2,2048,512]{2,1,0:T(8,128)(2,1)S(1)}, bf16[2,2048,512]{2,1,0:T(8,128)(2,1)}, u32[]{:S(2)}) copy-start(bf16[2,2048,512]{2,1,0:T(8,128)(2,1)} %get-tuple-element.29) | copy-start | bytes 12582916
  266.5 3.7 %copy-start.9 = (bf16[2,512,2048]{2,1,0:T(8,128)(2,1)S(1)}, bf16[2,512,2048]{2,1,0:T(8,128)(2,1)}, u32[]{:S(2)}) copy-start(bf16[2,512,2048]{2,1,0:T(8,128)(2,1)} %get-tuple-element.30) | copy-start | bytes 12582916

commit v4 on v3

v4 whole, which is shorter than its diff:
```python
import jax
import jax.numpy as jnp
import numpy as np
from jax import lax
from jax.experimental import pallas as pl
from jax.experimental.pallas import tpu as pltpu
from jax.sharding import PartitionSpec as P

TOP = 10
EPSILON = 1e-06
CAP = 6
BF = jnp.bfloat16
F32 = jnp.float32
VMEM_LIMIT = 62 * 2**20
MESH = pl.DeviceIdType.MESH
STRIDE = 37


def dot(a, b, ca=1, cb=0):
    return lax.dot_general(a, b, (((ca,), (cb,)), ((), ())), preferred_element_type=F32)


def order_in():
    m = np.zeros((192, 192), np.float32)
    for s in range(8):
        for h in range(2):
            for a in range(2):
                for r in range(CAP):
                    m[a * 96 + h * 48 + s * CAP + r, s * 24 + h * 12 + a * CAP + r] = 1
    return m


def order_out():
    m = np.zeros((192, 192), np.float32)
    for s in range(8):
        for q in range(4):
            for r in range(CAP):
                m[s * 24 + q * CAP + r, q * 48 + s * CAP + r] = 1
    return m


def place(n):
    v = ((n + 1) * STRIDE) % 128
    return v // 32, (v // 8) % 4, (v // 2) % 4, v % 2


def here():
    dp, seq = lax.axis_index("dp"), lax.axis_index("seq")
    return dp % 4, dp // 4, seq // 2, seq % 2


def device_at(n, sign):
    x, y, z, core = here()
    dx, dy, dz, dcore = place(n)
    x, y, z = (x + sign * dx + 4) % 4, (y + sign * dy + 4) % 4, (z + sign * dz + 4) % 4
    return y * 4 + x, z * 2 + (core + dcore) % 2


def core_kernel(
    ids_ref, w_ref, dest_ref, hid_ref, cot_ref, gain_in, gate, up, down, into_ref, out_of_ref, slot_ref, part_ref,
    hidden_ref, total_ref, back, ret, came, send, d_gate, d_up, d_down,
    tab_s, wt_s, src_s, pack_s, back_s, sum_s, gain_ref, gain_s, g_gate, g_up, g_down, raw_s, rows_s, norm_s, grad_s, act_s, gb_s, ub_s, ret_s, dw_s, dd_s,
    gsum_s, piece_s, arrive_s, share_s, share_in_s,
    pack_sem, w_sem, gain_send, gain_recv, f_send, f_recv, r_send, r_recv, load_sem, store_sem, dw_sem, t_send, t_recv,
):
    dp, seq = lax.axis_index("dp"), lax.axis_index("seq")
    devices = 128
    width = norm_s.shape[2]
    half, quarter = width // 2, width // 4
    group = 32
    rows = group * CAP

    def gain_copy(i):
        return pltpu.make_async_remote_copy(
            gain_in, gain_s.at[dp], gain_send, gain_recv, device_id=((dp + i) % 16, seq), device_id_type=MESH
        )

    own_gain = pltpu.make_async_copy(gain_in, gain_s.at[dp], gain_recv)
    own_gain.start()

    @pl.loop(1, 16)
    def _(i):
        gain_copy(i).start()

    loads = [
        pltpu.make_async_copy(gate, g_gate, w_sem.at[0]),
        pltpu.make_async_copy(up, g_up, w_sem.at[1]),
        pltpu.make_async_copy(down, g_down, w_sem.at[2]),
    ]
    for c in loads:
        c.start()

    def at(n, size=1):
        return pl.ds(pl.multiple_of(n * 24, 8), size * 24)

    tokens = hid_ref.shape[0]
    for h in range(2):
        src_s[h * 2 * tokens : h * 2 * tokens + tokens, :] = hid_ref[:, h * half : (h + 1) * half]
        src_s[h * 2 * tokens + tokens : (h + 1) * 2 * tokens, :] = cot_ref[:, h * half : (h + 1) * half]
    earlier = lax.broadcasted_iota(jnp.int32, (tokens, tokens), 0) < lax.broadcasted_iota(
        jnp.int32, (tokens, tokens), 1
    )
    before = jnp.where(earlier, 1.0, 0.0).astype(BF)
    for w in range(2):
        expert = jnp.broadcast_to(2 * dest_ref[...] + w, (devices, tokens))
        hit = jnp.zeros((devices, tokens), F32)
        weight = jnp.zeros((devices, tokens), F32)
        for k in range(TOP):
            same = ids_ref[k : k + 1, :] == expert
            hit = hit + jnp.where(same, 1.0, 0.0)
            weight = weight + jnp.where(same, w_ref[k : k + 1, :], 0.0)
        tab_s[w] = jnp.where(hit > 0.0, dot(hit.astype(BF), before), -1.0)
        wt_s[w] = weight

    block = 16
    shape = (block, 24, tokens)
    row = lax.broadcasted_iota(jnp.int32, shape, 1)
    in_half = jnp.where(row >= 12, 1, 0)
    row = row - 12 * in_half
    is_grad = jnp.where(row >= CAP, 1, 0)
    slot = (row - CAP * is_grad).astype(F32)
    kind = 2 * in_half + is_grad
    first = jnp.where(lax.broadcasted_iota(jnp.int32, shape, 2) == 0, 1.0, 0.0)

    def packed(t):
        return pltpu.make_async_copy(
            pack_s.at[t % 2], send.at[t // 8, at((t % 8) * block, block)], pack_sem.at[t % 2]
        )

    def go(t):
        packed(t).wait()
        w, low = t // 8, (t % 8) * block

        @pl.loop(low, jnp.minimum(low + block, devices - 1))
        def _(n):
            pltpu.make_async_remote_copy(
                send.at[w, at(n)],
                came.at[w, at(n)],
                f_send.at[w],
                f_recv.at[w * 4 + n // group],
                device_id=device_at(n, 1),
                device_id_type=MESH,
            ).start()

        @pl.when(t % 8 == 7)
        def _():
            last = at(devices - 1)
            pltpu.make_async_copy(send.at[w, last], came.at[w, last], f_recv.at[w * 4 + 3]).start()

    @pl.loop(0, 16)
    def _(t):
        w = t // 8
        these = pl.ds(pl.multiple_of((t % 8) * block, block), block)
        table = jnp.broadcast_to(tab_s[w, these, :][:, None, :], shape)
        weight = jnp.broadcast_to(wt_s[w, these, :][:, None, :], shape)
        pick = jnp.where(table == slot, 1.0, 0.0)
        scale = jnp.sum(jnp.where(is_grad == 1, pick * weight, first), axis=2, keepdims=True).reshape(block * 24, 1)
        pieces = [jnp.where(kind == m, pick, 0.0).reshape(block * 24, tokens).astype(BF) for m in range(4)]
        pack_s[t % 2] = (dot(jnp.concatenate(pieces, axis=1), src_s[...]) * scale).astype(BF)
        packed(t).start()

        @pl.when(t > 0)
        def _():
            go(t - 1)

    go(15)

    for c in loads:
        c.wait()
    pltpu.make_async_copy(gain_s, gain_s, gain_recv).wait()
    gain_ref[...] = jnp.concatenate([gain_s[i] for i in range(16)], axis=1)
    gsum_s[...] = jnp.zeros_like(gsum_s)

    @pl.loop(0, 8)
    def _(step):
        w, g = step // 4, step % 4
        slab = at(g * group, group)
        pltpu.make_async_copy(came.at[w, slab], came.at[w, slab], f_recv.at[step]).wait()
        load = pltpu.make_async_copy(came.at[w, slab], rows_s, load_sem)
        load.start()
        load.wait()
        mine = pl.ds(pl.multiple_of(g * rows, rows), rows)
        for b in range(4):
            moved = dot(into_ref[...], rows_s[b * 192 : (b + 1) * 192, :])
            there = pl.ds(pl.multiple_of(g * rows + b * 48, 16), 48)
            for h in range(2):
                raw_s[b * 48 : (b + 1) * 48, h * half : (h + 1) * half] = moved[h * 48 : (h + 1) * 48, :]
                grad_s[w, there, h * half : (h + 1) * half] = moved[96 + h * 48 : 96 + (h + 1) * 48, :].astype(BF)
        raw = raw_s[...]
        root = lax.rsqrt(jnp.mean(raw * raw, axis=1, keepdims=True) + EPSILON)
        normed = (raw * root * gain_ref[...]).astype(BF)
        norm_s[w, mine, :] = normed
        pre_gate = dot(normed, g_gate[w])
        pre_up = dot(normed, g_up[w])
        sig = jax.nn.sigmoid(pre_gate)
        silu = pre_gate * sig
        act_s[w, mine, :] = (silu * pre_up).astype(BF)
        grad_act = dot(grad_s[w, mine, :], g_down[w], 1, 1)
        gate_back = (grad_act * pre_up * sig * (1.0 + pre_gate * (1.0 - sig))).astype(BF)
        up_back = (grad_act * silu).astype(BF)
        gb_s[w, mine, :] = gate_back
        ub_s[w, mine, :] = up_back
        returned = (dot(gate_back, g_gate[w], 1, 1) + dot(up_back, g_up[w], 1, 1)).astype(BF)
        gsum_s[...] += jnp.sum(returned.astype(F32) * (raw_s[...] * root), axis=0, keepdims=True)
        for b in range(4):
            part = returned[b * 48 : (b + 1) * 48, :]
            stacked = jnp.concatenate([part[:, q * quarter : (q + 1) * quarter] for q in range(4)], axis=0)
            ret_s[b * 192 : (b + 1) * 192, :] = dot(out_of_ref[...], stacked).astype(BF)
        store = pltpu.make_async_copy(ret_s, ret.at[w, slab], store_sem)
        store.start()
        store.wait()

        @pl.loop(g * group, jnp.minimum(g * group + group, devices - 1))
        def _(n):
            pltpu.make_async_remote_copy(
                ret.at[w, at(n)],
                back.at[w, at(n)],
                r_send,
                r_recv.at[step],
                device_id=device_at(n, -1),
                device_id_type=MESH,
            ).start()

    for w in range(2):
        last = at(devices - 1)
        pltpu.make_async_copy(ret.at[w, last], back.at[w, last], r_recv.at[w * 4 + 3]).start()

    for p in range(16):
        piece_s[p] = gsum_s[:, p * 128 : (p + 1) * 128]

    def piece(i):
        return pltpu.make_async_remote_copy(
            piece_s.at[(dp + i) % 16], arrive_s.at[i], t_send.at[0], t_recv.at[0],
            device_id=((dp + i) % 16, seq), device_id_type=MESH,
        )

    @pl.loop(1, 16)
    def _(i):
        piece(i).start()

    wide = 256
    for w in range(2):
        if w == 1:
            for c in stores:
                c.wait()

        @pl.loop(0, width // wide)
        def _(j):
            lanes = pl.ds(pl.multiple_of(j * wide, wide), wide)
            left = norm_s[w, :, lanes]
            dw_s[0, lanes, :] = dot(left, gb_s[w], 0, 0).astype(BF)
            dw_s[1, lanes, :] = dot(left, ub_s[w], 0, 0).astype(BF)
            dd_s[:, lanes] = dot(act_s[w], grad_s[w, :, lanes], 0, 0).astype(BF)

        stores = [
            pltpu.make_async_copy(dw_s.at[0], d_gate.at[w], dw_sem.at[0]),
            pltpu.make_async_copy(dw_s.at[1], d_up.at[w], dw_sem.at[1]),
            pltpu.make_async_copy(dd_s, d_down.at[w], dw_sem.at[2]),
        ]
        for c in stores:
            c.start()

    fifteen = arrive_s.at[pl.ds(1, 15)]
    pltpu.make_async_copy(fifteen, fifteen, t_recv.at[0]).wait()
    share = piece_s[dp]
    for i in range(1, 16):
        share = share + arrive_s[i]
    share_s[...] = share

    def to_copy(i):
        return pltpu.make_async_remote_copy(
            share_s, share_in_s.at[i], t_send.at[1], t_recv.at[1], device_id=(dp, (seq + i) % 8), device_id_type=MESH
        )

    @pl.loop(1, 8)
    def _(i):
        to_copy(i).start()

    for c in stores:
        c.wait()

    sum_s[...] = jnp.zeros_like(sum_s)
    count = block * 24
    spread_at = lax.broadcasted_iota(jnp.int32, (block, count), 1) - 24 * lax.broadcasted_iota(
        jnp.int32, (block, count), 0
    )
    spread = jnp.where((spread_at >= 0) & (spread_at < 24), 1.0, 0.0).astype(BF)

    @pl.loop(0, 8)
    def _(step):
        w, g = step // 4, step % 4
        slab = at(g * group, group)
        pltpu.make_async_copy(back.at[w, slab], back.at[w, slab], r_recv.at[step]).wait()
        load = pltpu.make_async_copy(back.at[w, slab], back_s, load_sem)
        load.start()
        load.wait()
        for b in range(2):
            these = pl.ds(pl.multiple_of(g * group + b * block, block), block)
            table = dot(tab_s[w, these, :].astype(BF), spread, 0, 0)
            pick = jnp.where(table == slot_ref[...], 1.0, 0.0)
            left = jnp.concatenate(
                [jnp.where(part_ref[...] == float(q), pick, 0.0).astype(BF) for q in range(4)], axis=0
            )
            sum_s[...] += dot(left, back_s[b * count : (b + 1) * count, :])

    summed = jnp.concatenate([sum_s[q * tokens : (q + 1) * tokens, :] for q in range(4)], axis=1)
    raw = hid_ref[...].astype(F32)
    root = lax.rsqrt(jnp.mean(raw * raw, axis=1, keepdims=True) + EPSILON)
    scaled = raw * root
    gained = summed * gain_ref[...]
    centre = jnp.mean(gained * scaled, axis=1, keepdims=True)
    hidden_ref[...] = (cot_ref[...].astype(F32) + root * (gained - scaled * centre)).astype(BF)

    seven = share_in_s.at[pl.ds(1, 7)]
    pltpu.make_async_copy(seven, seven, t_recv.at[1]).wait()
    for i in range(1, 8):
        share = share + share_in_s[i]
    total_ref[...] = share

    most = at(0, devices - 1)
    for w in range(2):
        pltpu.make_async_copy(send.at[w, most], send.at[w, most], f_send.at[w]).wait()
        pltpu.make_async_copy(ret.at[w, most], ret.at[w, most], r_send).wait()
    pltpu.make_async_copy(fifteen, fifteen, t_send.at[0]).wait()
    pltpu.make_async_copy(seven, seven, t_send.at[1]).wait()
    pltpu.make_async_copy(gain_s.at[pl.ds(1, 15)], gain_s.at[pl.ds(1, 15)], gain_send).wait()


def core(ids_t, w_t, dest, hidden, cot, gain, gate, up, down):
    tokens, width = hidden.shape
    experts, _, deep = gate.shape
    devices = dest.shape[0]
    total = devices * 24
    slots, half = total // 4, width // 2
    hbm = pl.BlockSpec(memory_space=pl.ANY)
    vmem = pl.BlockSpec(memory_space=pltpu.VMEM)
    back = jax.ShapeDtypeStruct((2, total, width // 4), BF)
    rows = jax.ShapeDtypeStruct((2, total, half), BF)
    dma = pltpu.SemaphoreType.DMA
    place_in = np.arange(16 * 24) % 24
    slot = jnp.asarray((place_in % CAP)[None, :], F32)
    part = jnp.asarray((place_in // CAP)[None, :], F32)
    outs = pl.pallas_call(
        core_kernel,
        out_shape=[
            jax.ShapeDtypeStruct((tokens, width), BF),
            jax.ShapeDtypeStruct((1, 128), F32),
            back,
            back,
            rows,
            rows,
            jax.ShapeDtypeStruct(gate.shape, BF),
            jax.ShapeDtypeStruct(up.shape, BF),
            jax.ShapeDtypeStruct(down.shape, BF),
        ],
        in_specs=[vmem] * 5 + [hbm] * 4 + [vmem] * 4,
        out_specs=[vmem] * 2 + [hbm] * 7,
        scratch_shapes=[
            pltpu.VMEM((2, devices, tokens), F32),
            pltpu.VMEM((2, devices, tokens), F32),
            pltpu.VMEM((4 * tokens, half), BF),
            pltpu.VMEM((2, 16 * 24, half), BF),
            pltpu.VMEM((total // 4, width // 4), BF),
            pltpu.VMEM((4 * tokens, width // 4), F32),
            pltpu.VMEM((1, width), F32),
            pltpu.VMEM((16, 1, 128), F32),
            pltpu.VMEM(gate.shape, BF),
            pltpu.VMEM(up.shape, BF),
            pltpu.VMEM(down.shape, BF),
            pltpu.VMEM((slots // 4, width), F32),
            pltpu.VMEM((total // 4, half), BF),
            pltpu.VMEM((experts, slots, width), BF),
            pltpu.VMEM((experts, slots, width), BF),
            pltpu.VMEM((experts, slots, deep), BF),
            pltpu.VMEM((experts, slots, deep), BF),
            pltpu.VMEM((experts, slots, deep), BF),
            pltpu.VMEM((total // 4, width // 4), BF),
            pltpu.VMEM((2, width, deep), BF),
            pltpu.VMEM((deep, width), BF),
            pltpu.VMEM((1, width), F32),
            pltpu.VMEM((16, 1, 128), F32),
            pltpu.VMEM((16, 1, 128), F32),
            pltpu.VMEM((1, 128), F32),
            pltpu.VMEM((8, 1, 128), F32),
            dma((2,)), dma((3,)), dma, dma, dma((2,)), dma((8,)), dma, dma((8,)), dma, dma, dma((3,)), dma((2,)), dma((2,)),
        ],
        compiler_params=pltpu.CompilerParams(has_side_effects=True, vmem_limit_bytes=VMEM_LIMIT),
        cost_estimate=pl.CostEstimate(flops=60 * 10**9, bytes_accessed=80 * 10**6, transcendentals=10**6),
        name="core",
    )(
        ids_t, w_t, dest, hidden, cot, gain, gate, up, down,
        jnp.asarray(order_in(), BF), jnp.asarray(order_out(), BF), slot, part,
    )
    return outs[0], outs[1], outs[6], outs[7], outs[8]


def shards(
    hidden_in, cotangent, norm_gain, route_weights, expert_ids, expert_gate, expert_up, expert_down
):
    hidden, cot = hidden_in[0], cotangent[0]
    tokens, width = hidden.shape
    devices = lax.axis_size("dp") * lax.axis_size("seq")
    ids_t = expert_ids[0].T
    w_t = route_weights[0].T
    dp, seq = device_at(jnp.arange(devices, dtype=jnp.int32), 1)
    dest = (dp * 8 + seq).astype(jnp.int32).reshape(devices, 1)
    grad_hidden, grad_gain, grad_gate, grad_up, grad_down = core(
        ids_t, w_t, dest, hidden, cot, norm_gain.reshape(1, -1), expert_gate, expert_up, expert_down
    )
    return grad_hidden[None], grad_gain.reshape(-1), grad_gate, grad_up, grad_down


def solution(mesh):
    rows = P("dp", "seq", None)
    experts = P(("dp", "seq"), None, None)
    return jax.shard_map(
        shards,
        mesh=mesh,
        in_specs=(rows, rows, P("dp"), rows, rows, experts, experts, experts),
        out_specs=(rows, P("dp"), experts, experts, experts),
        check_vma=False,
    )
```

time: 273 us -> 261 us (0.956)
  Pallas kernels: 250 us -> 243 us
  local copies, waits for them, and re-layouts: 21.4 us -> 16 us
    pallas_call x3 -> x1, Pallas kernels: 250 us -> 243 us  [core(): pl.pallas_call(core_kernel, out_shape=[jax.ShapeDtypeStruct((tokens, widt...]
    unnamed x32 -> x11, local copies, waits for them, and re-layouts: 21.4 us -> 16 us
where the time goes in v4:
time: 261 us
  Pallas kernels  243 us (93%)
  local copies, waits for them, and re-layouts  16 us (6%)
    pallas_call x1, Pallas kernels, core(): pl.pallas_call(core_kernel, out_shape=[jax.ShapeDtypeStruct((tokens, widt...  243 us
    unnamed x11, local copies, waits for them, and re-layouts  16 us

profile of v4, /device:TPU:1, one launch (start us, length us, event | category | flops | bytes accessed | tf_op | source)
XLA Modules:
  0.0 260.6 jit_solution(13828942029275894636)
XLA Ops:
  0.7 1.3 copy.21
  2.0 1.3 copy.22
  3.2 0.9 fusion.9.dest_ref
  4.2 243.0 %core.1 = (bf16[128,2048]{1,0:T(8,128)(2,1)}, f32[1,128]{1,0:T(1,128)}, bf16[2,3072,512]{2,1,0:T(8,128)(2,1)}, bf16[2,3072,512]{2,1,0:T(8,128)(2,1)}, bf16[2,307...) custom-call(s32[10,128]{1,0:T(8,128)} %bitcast.17, ...), custom_call_target="tpu_custom_call" | custom-call | flops 60000002048 | bytes 80000000 | tf_op jit(solution)/shard_map/core/pallas_call | solution.py:343
  247.2 1.9 copy.28
  249.1 1.2 copy.29
  250.2 0.0 copy-start.1
  250.2 4.6 %copy.30 = bf16[2,2048,512]{2,1,0:T(8,128)(2,1)} copy(bf16[2,2048,512]{2,1,0:T(8,128)(2,1)} %get-tuple-element.22) | data formatting | bytes 8388608
  254.9 0.0 copy-done.1
  254.9 0.0 copy-start
  254.9 2.1 copy.31
  257.0 1.6 copy-done
  258.6 2.0 copy.32
Async XLA Ops:
  250.2 4.6 %copy-start.1 = (bf16[2,2048,512]{2,1,0:T(8,128)(2,1)S(1)}, bf16[2,2048,512]{2,1,0:T(8,128)(2,1)}, u32[]{:S(2)}) copy-start(bf16[2,2048,512]{2,1,0:T(8,128)(2,1)} %get-tuple-element.23) | copy-start | bytes 12582916
  254.9 3.7 %copy-start = (bf16[2,512,2048]{2,1,0:T(8,128)(2,1)S(1)}, bf16[2,512,2048]{2,1,0:T(8,128)(2,1)}, u32[]{:S(2)}) copy-start(bf16[2,512,2048]{2,1,0:T(8,128)(2,1)} %get-tuple-element.24) | copy-start | bytes 12582916

commit v5 on v4

v5 whole, which is shorter than its diff:
```python
import jax
import jax.numpy as jnp
import numpy as np
from jax import lax
from jax.experimental import pallas as pl
from jax.experimental.pallas import tpu as pltpu
from jax.sharding import PartitionSpec as P

TOP = 10
EPSILON = 1e-06
CAP = 6
BF = jnp.bfloat16
F32 = jnp.float32
VMEM_LIMIT = 63 * 2**20
MESH = pl.DeviceIdType.MESH
PART = ((0, 640), (640, 640), (1280, 768))
PLANE = ((1, 2), (0, 2), (0, 1))
LINE = 4 * CAP
ROWS = 16 * LINE
CHUNKS = 4


def dot(a, b, ca=1, cb=0):
    return lax.dot_general(a, b, (((ca,), (cb,)), ((), ())), preferred_element_type=F32)


def device_at(shift, core):
    dp, seq = lax.axis_index("dp"), lax.axis_index("seq")
    x, y, z = (dp + shift[0] + 4) % 4, (dp // 4 + shift[1] + 4) % 4, (seq // 2 + shift[2] + 4) % 4
    return y * 4 + x, z * 2 + (seq + core) % 2


def along(a, m):
    return tuple(m if i == a else 0 for i in range(3))


def across(a, p, sign):
    shift = [0, 0, 0]
    shift[PLANE[a][0]] = sign * (p // 4)
    shift[PLANE[a][1]] = sign * (p % 4)
    return tuple(shift)


def order(a):
    matrix = np.zeros((ROWS, ROWS), np.float32)
    for p in range(16):
        for m in range(4):
            at = [0, 0, 0]
            at[PLANE[a][0]], at[PLANE[a][1]], at[a] = p // 4, p % 4, m
            for j in range(CAP):
                matrix[(at[0] * 16 + at[1] * 4 + at[2]) * CAP + j, p * LINE + m * CAP + j] = 1
    return matrix


def core_kernel(
    meta_ref, dest_ref, hid_ref, cot_ref, gain_in, gate, up, down, order_ref, slot_ref, part_ref,
    hidden_ref, total_ref,
    send0, send1, send2, came0, came1, came2, ret0, ret1, ret2, back0, back1, back2, d_gate, d_up, d_down,
    meta_s, tab_s, wt_s, row0, row1, row2, cot0, cot1, cot2, pack0, pack1, pack2, in0, in1, in2, sum0, sum1, sum2,
    near0, near1, near2,
    gain_ref, gain_s, g_gate, g_up, g_down, raw_s, norm_s, grad_s, act_s, gb_s, ub_s,
    gsum_s, piece_s, arrive_s, share_s, share_in_s,
    ag_send, ag_recv, pack_sem, w_sem, gain_send, gain_recv, f_send, f_recv, r_send, r_recv, load_sem, dw_sem,
    t_send, t_recv, l_send, l_recv,
):
    dp, seq = lax.axis_index("dp"), lax.axis_index("seq")
    send, came, ret, back = (send0, send1, send2), (came0, came1, came2), (ret0, ret1, ret2), (back0, back1, back2)
    line_rows, line_cots, pack = (row0, row1, row2), (cot0, cot1, cot2), (pack0, pack1, pack2)
    into, sums, near = (in0, in1, in2), (sum0, sum1, sum2), (near0, near1, near2)
    tokens, width = hid_ref.shape

    for m in (2, 1, 3):
        for a in range(3):
            target = dict(device_id=device_at(along(a, m), 0), device_id_type=MESH)
            lanes = pl.ds(*PART[a])
            pltpu.make_async_remote_copy(meta_ref, meta_s.at[a, m], ag_send.at[3 * a + 0], ag_recv.at[3 * a + 0], **target).start()
            pltpu.make_async_remote_copy(hid_ref.at[:, lanes], line_rows[a].at[m], ag_send.at[3 * a + 1], ag_recv.at[3 * a + 1], **target).start()
            pltpu.make_async_remote_copy(cot_ref.at[:, lanes], line_cots[a].at[m], ag_send.at[3 * a + 2], ag_recv.at[3 * a + 2], **target).start()

    def gain_copy(i):
        return pltpu.make_async_remote_copy(
            gain_in, gain_s.at[dp], gain_send, gain_recv, device_id=((dp + i) % 16, seq), device_id_type=MESH
        )

    own_gain = pltpu.make_async_copy(gain_in, gain_s.at[dp], gain_recv)
    own_gain.start()

    @pl.loop(1, 16)
    def _(i):
        gain_copy(i).start()

    loads = [
        pltpu.make_async_copy(gate, g_gate, w_sem.at[0]),
        pltpu.make_async_copy(up, g_up, w_sem.at[1]),
        pltpu.make_async_copy(down, g_down, w_sem.at[2]),
    ]
    for c in loads:
        c.start()

    earlier = lax.broadcasted_iota(jnp.int32, (tokens, tokens), 0) < lax.broadcasted_iota(
        jnp.int32, (tokens, tokens), 1
    )
    before = jnp.where(earlier, 1.0, 0.0).astype(BF)
    for a in range(3):
        lanes = slice(PART[a][0], PART[a][0] + PART[a][1])
        meta_s[a, 0] = meta_ref[...]
        line_rows[a][0] = hid_ref[:, lanes]
        line_cots[a][0] = cot_ref[:, lanes]
    three = pl.ds(1, 3)
    for a in range(3):
        for n, ref in enumerate((meta_s.at[a, three], line_rows[a].at[three], line_cots[a].at[three])):
            pltpu.make_async_copy(ref, ref, ag_recv.at[3 * a + n]).wait()
        expert = jnp.broadcast_to(dest_ref[a], (CHUNKS * 16, tokens))
        for m in range(4):
            hit = jnp.zeros((CHUNKS * 16, tokens), F32)
            weight = jnp.zeros((CHUNKS * 16, tokens), F32)
            for k in range(TOP):
                same = meta_s[a, m, k : k + 1, :] == expert
                hit = hit + jnp.where(same, 1.0, 0.0)
                weight = weight + jnp.where(same, meta_s[a, m, 12 + k : 13 + k, :], 0.0)
            tab_s[a, m] = jnp.where(hit > 0.0, dot(hit.astype(BF), before), -1.0)
            wt_s[a, m] = weight

    def at(p, size=1):
        return pl.ds(pl.multiple_of(p * LINE, 8), size * LINE)

    shape = (16, LINE, tokens)
    row = lax.broadcasted_iota(jnp.int32, shape, 1)
    member = sum(jnp.where(row >= m * CAP, 1, 0) for m in range(1, 4))
    slot = (row - CAP * member).astype(F32)

    def forth(a, c, p):
        return pltpu.make_async_remote_copy(
            send[a].at[c, :, at(p)], came[a].at[c, :, at(p)], f_send.at[c * 3 + a], f_recv.at[c * 3 + a],
            device_id=device_at(across(a, p, 1), c % 2), device_id_type=MESH,
        )

    def forth_again(a, c, p):
        return pltpu.make_async_remote_copy(
            ret[a].at[c, at(p)], back[a].at[c, at(p)], r_send.at[c * 3 + a], r_recv.at[c * 3 + a],
            device_id=device_at(across(a, p, -1), c % 2), device_id_type=MESH,
        )

    def scattered(i):
        return ((i + 1) * 5) % 16

    @pl.loop(0, CHUNKS)
    def _(c):
        these = pl.ds(pl.multiple_of(c * 16, 16), 16)
        for a in range(3):
            pieces, scale = [], jnp.zeros((16, LINE, 1), F32)
            for m in range(4):
                table = jnp.broadcast_to(tab_s[a, m, these, :][:, None, :], shape)
                weight = jnp.broadcast_to(wt_s[a, m, these, :][:, None, :], shape)
                pick = jnp.where((member == m) & (table == slot), 1.0, 0.0)
                scale = scale + jnp.sum(pick * weight, axis=2, keepdims=True)
                pieces.append(pick.reshape(ROWS, tokens).astype(BF))
            left = jnp.concatenate(pieces, axis=1)
            size = PART[a][1]
            pack[a][0] = dot(left, line_rows[a][...].reshape(4 * tokens, size)).astype(BF)
            pack[a][1] = (dot(left, line_cots[a][...].reshape(4 * tokens, size)) * scale.reshape(ROWS, 1)).astype(BF)
            pltpu.make_async_copy(pack[a], send[a].at[c], pack_sem.at[a]).start()
        for a in range(3):
            pltpu.make_async_copy(pack[a], send[a].at[c], pack_sem.at[a]).wait()

        @pl.loop(0, 15)
        def _(i):
            for a in range(3):
                forth(a, c, scattered(i)).start()

        @pl.when(c % 2 == 1)
        def _():
            for a in range(3):
                forth(a, c, 0).start()

        @pl.when(c % 2 == 0)
        def _():
            for a in range(3):
                pltpu.make_async_copy(send[a].at[c, :, at(0)], came[a].at[c, :, at(0)], f_recv.at[c * 3 + a]).start()

    for c in loads:
        c.wait()
    pltpu.make_async_copy(gain_s, gain_s, gain_recv).wait()
    gain_ref[...] = jnp.concatenate([gain_s[i] for i in range(16)], axis=1)
    gsum_s[...] = jnp.zeros_like(gsum_s)
    wide = 256

    @pl.loop(0, CHUNKS)
    def _(c):
        w = c // 2
        for a in range(3):
            pltpu.make_async_copy(came[a].at[c], came[a].at[c], f_recv.at[c * 3 + a]).wait()
        for a in range(3):
            pltpu.make_async_copy(came[a].at[c], into[a], load_sem.at[a]).start()
        mine = pl.ds(pl.multiple_of((c % 2) * ROWS, ROWS), ROWS)
        for a in range(3):
            pltpu.make_async_copy(came[a].at[c], into[a], load_sem.at[a]).wait()
            lanes = slice(PART[a][0], PART[a][0] + PART[a][1])
            raw_s[:, lanes] = dot(order_ref[a], into[a][0])
            grad_s[w, mine, lanes] = dot(order_ref[a], into[a][1]).astype(BF)
        root = lax.rsqrt(jnp.mean(raw_s[...] * raw_s[...], axis=1, keepdims=True) + EPSILON)
        norm_s[w, mine, :] = (raw_s[...] * root * gain_ref[...]).astype(BF)
        pre_gate = dot(norm_s[w, mine, :], g_gate[w])
        pre_up = dot(norm_s[w, mine, :], g_up[w])
        sig = jax.nn.sigmoid(pre_gate)
        silu = pre_gate * sig
        act_s[w, mine, :] = (silu * pre_up).astype(BF)
        grad_act = dot(grad_s[w, mine, :], g_down[w], 1, 1)
        gb_s[w, mine, :] = (grad_act * pre_up * sig * (1.0 + pre_gate * (1.0 - sig))).astype(BF)
        ub_s[w, mine, :] = (grad_act * silu).astype(BF)
        for a in range(3):
            lanes = slice(PART[a][0], PART[a][0] + PART[a][1])
            returned = (
                dot(gb_s[w, mine, :], g_gate[w, lanes, :], 1, 1) + dot(ub_s[w, mine, :], g_up[w, lanes, :], 1, 1)
            ).astype(BF)
            gsum_s[:, lanes] += jnp.sum(returned.astype(F32) * (raw_s[:, lanes] * root), axis=0, keepdims=True)
            pack[a][0] = dot(order_ref[a], returned, 0, 0).astype(BF)
            pltpu.make_async_copy(pack[a].at[0], ret[a].at[c], pack_sem.at[a]).start()
        for a in range(3):
            pltpu.make_async_copy(pack[a].at[0], ret[a].at[c], pack_sem.at[a]).wait()

        @pl.loop(0, 15)
        def _(i):
            for a in range(3):
                forth_again(a, c, scattered(i)).start()

        @pl.when(c % 2 == 1)
        def _():
            for a in range(3):
                forth_again(a, c, 0).start()

            @pl.loop(0, width // wide)
            def _(j):
                lanes = pl.ds(pl.multiple_of(j * wide, wide), wide)
                left = norm_s[w, :, lanes]
                g_gate[w, lanes, :] = dot(left, gb_s[w], 0, 0).astype(BF)
                g_up[w, lanes, :] = dot(left, ub_s[w], 0, 0).astype(BF)
                g_down[w, :, lanes] = dot(act_s[w], grad_s[w, :, lanes], 0, 0).astype(BF)

            for n, (here, there) in enumerate(((g_gate, d_gate), (g_up, d_up), (g_down, d_down))):
                pltpu.make_async_copy(here.at[w], there.at[w], dw_sem.at[w * 3 + n]).start()

        @pl.when(c % 2 == 0)
        def _():
            for a in range(3):
                pltpu.make_async_copy(ret[a].at[c, at(0)], back[a].at[c, at(0)], r_recv.at[c * 3 + a]).start()

    for p in range(16):
        piece_s[p] = gsum_s[:, p * 128 : (p + 1) * 128]

    def piece(i):
        return pltpu.make_async_remote_copy(
            piece_s.at[(dp + i) % 16], arrive_s.at[i], t_send.at[0], t_recv.at[0],
            device_id=((dp + i) % 16, seq), device_id_type=MESH,
        )

    @pl.loop(1, 16)
    def _(i):
        piece(i).start()

    for a in range(3):
        sums[a][...] = jnp.zeros_like(sums[a])
    spread_at = lax.broadcasted_iota(jnp.int32, (16, ROWS), 1) - LINE * lax.broadcasted_iota(jnp.int32, (16, ROWS), 0)
    spread = jnp.where((spread_at >= 0) & (spread_at < LINE), 1.0, 0.0).astype(BF)

    @pl.loop(0, CHUNKS)
    def _(c):
        these = pl.ds(pl.multiple_of(c * 16, 16), 16)
        for a in range(3):
            pltpu.make_async_copy(back[a].at[c], back[a].at[c], r_recv.at[c * 3 + a]).wait()
        for a in range(3):
            pltpu.make_async_copy(back[a].at[c], into[a].at[0], load_sem.at[a]).start()
        for a in range(3):
            pieces = []
            for m in range(4):
                table = dot(tab_s[a, m, these, :].astype(BF), spread, 0, 0)
                pieces.append(
                    jnp.where((part_ref[...] == float(m)) & (table == slot_ref[...]), 1.0, 0.0).astype(BF)
                )
            left = jnp.concatenate(pieces, axis=0)
            pltpu.make_async_copy(back[a].at[c], into[a].at[0], load_sem.at[a]).wait()
            sums[a][...] += dot(left, into[a][0])

    for a in range(3):
        line_rows[a][...] = sums[a][...].reshape(4, tokens, PART[a][1]).astype(BF)
    for m in (2, 1, 3):
        for a in range(3):
            pltpu.make_async_remote_copy(
                line_rows[a].at[m], near[a].at[m], l_send.at[a], l_recv.at[a],
                device_id=device_at(along(a, -m), 0), device_id_type=MESH,
            ).start()

    fifteen = arrive_s.at[pl.ds(1, 15)]
    pltpu.make_async_copy(fifteen, fifteen, t_recv.at[0]).wait()
    share = piece_s[dp]
    for i in range(1, 16):
        share = share + arrive_s[i]
    share_s[...] = share

    def to_copy(i):
        return pltpu.make_async_remote_copy(
            share_s, share_in_s.at[i], t_send.at[1], t_recv.at[1], device_id=(dp, (seq + i) % 8), device_id_type=MESH
        )

    @pl.loop(1, 8)
    def _(i):
        to_copy(i).start()

    for a in range(3):
        pltpu.make_async_copy(near[a].at[three], near[a].at[three], l_recv.at[a]).wait()
    summed = jnp.concatenate(
        [
            sums[a][0:tokens, :] + near[a][1].astype(F32) + near[a][2].astype(F32) + near[a][3].astype(F32)
            for a in range(3)
        ],
        axis=1,
    )
    raw = hid_ref[...].astype(F32)
    root = lax.rsqrt(jnp.mean(raw * raw, axis=1, keepdims=True) + EPSILON)
    scaled = raw * root
    gained = summed * gain_ref[...]
    centre = jnp.mean(gained * scaled, axis=1, keepdims=True)
    hidden_ref[...] = (cot_ref[...].astype(F32) + root * (gained - scaled * centre)).astype(BF)

    seven = share_in_s.at[pl.ds(1, 7)]
    pltpu.make_async_copy(seven, seven, t_recv.at[1]).wait()
    for i in range(1, 8):
        share = share + share_in_s[i]
    total_ref[...] = share

    for w in range(2):
        for n, (here, there) in enumerate(((g_gate, d_gate), (g_up, d_up), (g_down, d_down))):
            pltpu.make_async_copy(here.at[w], there.at[w], dw_sem.at[w * 3 + n]).wait()
    for a in range(3):
        for n, ref in enumerate((meta_s.at[a, three], line_rows[a].at[three], line_cots[a].at[three])):
            pltpu.make_async_copy(ref, ref, ag_send.at[3 * a + n]).wait()
        pltpu.make_async_copy(near[a].at[three], near[a].at[three], l_send.at[a]).wait()
        for c in range(CHUNKS):
            sent = at(0, 16) if c % 2 == 1 else at(1, 15)
            pltpu.make_async_copy(send[a].at[c, :, sent], send[a].at[c, :, sent], f_send.at[c * 3 + a]).wait()
            pltpu.make_async_copy(ret[a].at[c, sent], ret[a].at[c, sent], r_send.at[c * 3 + a]).wait()
    pltpu.make_async_copy(fifteen, fifteen, t_send.at[0]).wait()
    pltpu.make_async_copy(seven, seven, t_send.at[1]).wait()
    pltpu.make_async_copy(gain_s.at[pl.ds(1, 15)], gain_s.at[pl.ds(1, 15)], gain_send).wait()


def core(meta, dest, hidden, cot, gain, gate, up, down):
    tokens, width = hidden.shape
    experts, _, deep = gate.shape
    slots = 2 * ROWS
    hbm = pl.BlockSpec(memory_space=pl.ANY)
    vmem = pl.BlockSpec(memory_space=pltpu.VMEM)
    dma = pltpu.SemaphoreType.DMA
    sizes = [size for _, size in PART]
    shape = jax.ShapeDtypeStruct
    pairs = [shape((CHUNKS, 2, ROWS, size), BF) for size in sizes]
    singles = [shape((CHUNKS, ROWS, size), BF) for size in sizes]
    place = np.arange(ROWS) % LINE
    slot = jnp.asarray((place % CAP)[None, :], F32)
    part = jnp.asarray((place // CAP)[None, :], F32)
    line = [pltpu.VMEM((4, tokens, size), BF) for size in sizes]
    both = [pltpu.VMEM((2, ROWS, size), BF) for size in sizes]
    outs = pl.pallas_call(
        core_kernel,
        out_shape=[shape((tokens, width), BF), shape((1, 128), F32)]
        + pairs * 2
        + singles * 2
        + [shape(gate.shape, BF), shape(up.shape, BF), shape(down.shape, BF)],
        in_specs=[vmem] * 4 + [hbm] * 4 + [vmem] * 3,
        out_specs=[vmem] * 2 + [hbm] * 15,
        scratch_shapes=[
            pltpu.VMEM((3, 4, 24, tokens), F32),
            pltpu.VMEM((3, 4, CHUNKS * 16, tokens), F32),
            pltpu.VMEM((3, 4, CHUNKS * 16, tokens), F32),
        ]
        + line * 2
        + both * 2
        + [pltpu.VMEM((4 * tokens, size), F32) for size in sizes]
        + line
        + [
            pltpu.VMEM((1, width), F32),
            pltpu.VMEM((16, 1, 128), F32),
            pltpu.VMEM(gate.shape, BF),
            pltpu.VMEM(up.shape, BF),
            pltpu.VMEM(down.shape, BF),
            pltpu.VMEM((ROWS, width), F32),
            pltpu.VMEM((experts, slots, width), BF),
            pltpu.VMEM((experts, slots, width), BF),
            pltpu.VMEM((experts, slots, deep), BF),
            pltpu.VMEM((experts, slots, deep), BF),
            pltpu.VMEM((experts, slots, deep), BF),
            pltpu.VMEM((1, width), F32),
            pltpu.VMEM((16, 1, 128), F32),
            pltpu.VMEM((16, 1, 128), F32),
            pltpu.VMEM((1, 128), F32),
            pltpu.VMEM((8, 1, 128), F32),
            dma((9,)), dma((9,)), dma((3,)), dma((3,)), dma, dma, dma((12,)), dma((12,)), dma((12,)), dma((12,)),
            dma((3,)), dma((6,)), dma((2,)), dma((2,)), dma((3,)), dma((3,)),
        ],
        compiler_params=pltpu.CompilerParams(has_side_effects=True, vmem_limit_bytes=VMEM_LIMIT),
        cost_estimate=pl.CostEstimate(flops=60 * 10**9, bytes_accessed=80 * 10**6, transcendentals=10**6),
        name="core",
    )(
        meta, dest, hidden, cot, gain, gate, up, down,
        jnp.asarray(np.stack([order(a) for a in range(3)]), BF), slot, part,
    )
    return outs[0], outs[1], outs[-3], outs[-2], outs[-1]


def shards(
    hidden_in, cotangent, norm_gain, route_weights, expert_ids, expert_gate, expert_up, expert_down
):
    zeros = jnp.zeros((2, hidden_in.shape[1]), F32)
    meta = jnp.concatenate([expert_ids[0].T.astype(F32), zeros, route_weights[0].T, zeros], axis=0)
    n = jnp.arange(CHUNKS * 16, dtype=jnp.int32)
    dest = []
    for a in range(3):
        dp, seq = device_at(across(a, n % 16, 1), (n // 16) % 2)
        dest.append(2 * (dp * 8 + seq) + n // 32)
    dest = jnp.stack(dest).astype(F32)[:, :, None]
    grad_hidden, grad_gain, grad_gate, grad_up, grad_down = core(
        meta, dest, hidden_in[0], cotangent[0], norm_gain.reshape(1, -1), expert_gate, expert_up, expert_down
    )
    return grad_hidden[None], grad_gain.reshape(-1), grad_gate, grad_up, grad_down


def solution(mesh):
    rows = P("dp", "seq", None)
    experts = P(("dp", "seq"), None, None)
    return jax.shard_map(
        shards,
        mesh=mesh,
        in_specs=(rows, rows, P("dp"), rows, rows, experts, experts, experts),
        out_specs=(rows, P("dp"), experts, experts, experts),
        check_vma=False,
    )
```

time: 261 us -> 219 us (0.84)
  Pallas kernels: 243 us -> 200 us
    pallas_call x1, Pallas kernels: 243 us -> 200 us  [core(): pl.pallas_call(core_kernel, out_shape=[shape((tokens, width), BF), shape(...]
    unnamed x11 -> x10, local copies, waits for them, and re-layouts: 16 us -> 14.1 us
where the time goes in v5:
time: 219 us; the launch traced here: 217 us
  Pallas kernels  200 us (91%)
  local copies, waits for them, and re-layouts  14.9 us (7%)
    pallas_call x1, Pallas kernels, core(): pl.pallas_call(core_kernel, out_shape=[shape((tokens, width), BF), shape(...  200 us
    unnamed x10, local copies, waits for them, and re-layouts  14.1 us

profile of v5, /device:TPU:1, one launch (start us, length us, event | category | flops | bytes accessed | tf_op | source)
XLA Modules:
  0.0 217.3 jit_solution(16700853196446398430)
XLA Ops:
  0.8 0.7 copy.29
  1.5 0.7 fusion
  2.2 0.6 pad_maximum_fusion.meta_ref
  2.8 0.8 copy.23.dest_ref
  3.5 200.4 %core.1 = (bf16[128,2048]{1,0:T(8,128)(2,1)}, f32[1,128]{1,0:T(1,128)}, bf16[4,2,384,640]{3,2,1,0:T(8,128)(2,1)}, bf16[4,2,384,640]{3,2,1,0:T(8,128)(2,1)}, bf16...) custom-call(f32[24,128]{1,0:T(8,128)} %pad_maximum_fusion.meta_ref, ...), custom_call_target="tpu_custom_call" | custom-call | flops 60000002048 | bytes 80000000 | tf_op jit(solution)/shard_map/core/pallas_call | solution.py:363
  203.9 1.9 copy.35
  205.8 1.2 copy.36
  207.0 0.0 copy-start.1
  207.0 4.6 %copy.37 = bf16[2,2048,512]{2,1,0:T(8,128)(2,1)} copy(bf16[2,2048,512]{2,1,0:T(8,128)(2,1)} %get-tuple-element.24) | data formatting | bytes 8388608
  211.6 0.0 copy-done.1
  211.6 0.0 copy-start
  211.6 2.1 copy.38
  213.8 1.6 copy-done
  215.3 2.0 copy.39
  (4 shorter events, 0.1 us)
Async XLA Ops:
  207.0 4.6 %copy-start.1 = (bf16[2,2048,512]{2,1,0:T(8,128)(2,1)S(1)}, bf16[2,2048,512]{2,1,0:T(8,128)(2,1)}, u32[]{:S(2)}) copy-start(bf16[2,2048,512]{2,1,0:T(8,128)(2,1)} %get-tuple-element.25) | copy-start | bytes 12582916
  211.6 3.7 %copy-start = (bf16[2,512,2048]{2,1,0:T(8,128)(2,1)S(1)}, bf16[2,512,2048]{2,1,0:T(8,128)(2,1)}, u32[]{:S(2)}) copy-start(bf16[2,512,2048]{2,1,0:T(8,128)(2,1)} %get-tuple-element.26) | copy-start | bytes 12582916

commit v6 on v5

--- a/solution.py
+++ b/solution.py
@@ -16,6 +16,7 @@
 PART = ((0, 640), (640, 640), (1280, 768))
 PLANE = ((1, 2), (0, 2), (0, 1))
 LINE = 4 * CAP
+BOTH = pl.ds(0, 2)
 ROWS = 16 * LINE
 CHUNKS = 4
 
@@ -54,11 +55,11 @@
 
 def core_kernel(
     meta_ref, dest_ref, hid_ref, cot_ref, gain_in, gate, up, down, order_ref, slot_ref, part_ref,
-    hidden_ref, total_ref,
+    summed_ref, gain_ref, total_ref,
     send0, send1, send2, came0, came1, came2, ret0, ret1, ret2, back0, back1, back2, d_gate, d_up, d_down,
     meta_s, tab_s, wt_s, row0, row1, row2, cot0, cot1, cot2, pack0, pack1, pack2, in0, in1, in2, sum0, sum1, sum2,
     near0, near1, near2,
-    gain_ref, gain_s, g_gate, g_up, g_down, raw_s, norm_s, grad_s, act_s, gb_s, ub_s,
+    gain_s, g_gate, g_up, g_down, raw_s, norm_s, grad_s, act_s, gb_s, ub_s,
     gsum_s, piece_s, arrive_s, share_s, share_in_s,
     ag_send, ag_recv, pack_sem, w_sem, gain_send, gain_recv, f_send, f_recv, r_send, r_recv, load_sem, dw_sem,
     t_send, t_recv, l_send, l_recv,
@@ -72,10 +73,14 @@
     for m in (2, 1, 3):
         for a in range(3):
             target = dict(device_id=device_at(along(a, m), 0), device_id_type=MESH)
-            lanes = pl.ds(*PART[a])
             pltpu.make_async_remote_copy(meta_ref, meta_s.at[a, m], ag_send.at[3 * a + 0], ag_recv.at[3 * a + 0], **target).start()
-            pltpu.make_async_remote_copy(hid_ref.at[:, lanes], line_rows[a].at[m], ag_send.at[3 * a + 1], ag_recv.at[3 * a + 1], **target).start()
-            pltpu.make_async_remote_copy(cot_ref.at[:, lanes], line_cots[a].at[m], ag_send.at[3 * a + 2], ag_recv.at[3 * a + 2], **target).start()
+    for n, (source, lines) in enumerate(((hid_ref, line_rows), (cot_ref, line_cots))):
+        for m in (2, 1, 3):
+            for a in range(3):
+                pltpu.make_async_remote_copy(
+                    source.at[:, pl.ds(*PART[a])], lines[a].at[m], ag_send.at[3 * a + 1 + n], ag_recv.at[3 * a + 1 + n],
+                    device_id=device_at(along(a, m), 0), device_id_type=MESH,
+                ).start()
 
     def gain_copy(i):
         return pltpu.make_async_remote_copy(
@@ -107,9 +112,12 @@
         line_rows[a][0] = hid_ref[:, lanes]
         line_cots[a][0] = cot_ref[:, lanes]
     three = pl.ds(1, 3)
-    for a in range(3):
-        for n, ref in enumerate((meta_s.at[a, three], line_rows[a].at[three], line_cots[a].at[three])):
-            pltpu.make_async_copy(ref, ref, ag_recv.at[3 * a + n]).wait()
+
+    def landed(a, n, ref):
+        pltpu.make_async_copy(ref, ref, ag_recv.at[3 * a + n]).wait()
+
+    for a in range(3):
+        landed(a, 0, meta_s.at[a, three])
         expert = jnp.broadcast_to(dest_ref[a], (CHUNKS * 16, tokens))
         for m in range(4):
             hit = jnp.zeros((CHUNKS * 16, tokens), F32)
@@ -120,7 +128,6 @@
                 weight = weight + jnp.where(same, meta_s[a, m, 12 + k : 13 + k, :], 0.0)
             tab_s[a, m] = jnp.where(hit > 0.0, dot(hit.astype(BF), before), -1.0)
             wt_s[a, m] = weight
-
     def at(p, size=1):
         return pl.ds(pl.multiple_of(p * LINE, 8), size * LINE)
 
@@ -129,9 +136,9 @@
     member = sum(jnp.where(row >= m * CAP, 1, 0) for m in range(1, 4))
     slot = (row - CAP * member).astype(F32)
 
-    def forth(a, c, p):
+    def forth(a, c, p, kinds):
         return pltpu.make_async_remote_copy(
-            send[a].at[c, :, at(p)], came[a].at[c, :, at(p)], f_send.at[c * 3 + a], f_recv.at[c * 3 + a],
+            send[a].at[c, kinds, at(p)], came[a].at[c, kinds, at(p)], f_send.at[c * 3 + a], f_recv.at[c * 3 + a],
             device_id=device_at(across(a, p, 1), c % 2), device_id_type=MESH,
         )
 
@@ -142,41 +149,67 @@
         )
 
     def scattered(i):
-        return ((i + 1) * 5) % 16
-
-    @pl.loop(0, CHUNKS)
-    def _(c):
+        return ((i + 1) * 7) % 16
+
+    def picked(a, c):
         these = pl.ds(pl.multiple_of(c * 16, 16), 16)
-        for a in range(3):
-            pieces, scale = [], jnp.zeros((16, LINE, 1), F32)
-            for m in range(4):
-                table = jnp.broadcast_to(tab_s[a, m, these, :][:, None, :], shape)
-                weight = jnp.broadcast_to(wt_s[a, m, these, :][:, None, :], shape)
-                pick = jnp.where((member == m) & (table == slot), 1.0, 0.0)
-                scale = scale + jnp.sum(pick * weight, axis=2, keepdims=True)
-                pieces.append(pick.reshape(ROWS, tokens).astype(BF))
-            left = jnp.concatenate(pieces, axis=1)
-            size = PART[a][1]
-            pack[a][0] = dot(left, line_rows[a][...].reshape(4 * tokens, size)).astype(BF)
-            pack[a][1] = (dot(left, line_cots[a][...].reshape(4 * tokens, size)) * scale.reshape(ROWS, 1)).astype(BF)
-            pltpu.make_async_copy(pack[a], send[a].at[c], pack_sem.at[a]).start()
-        for a in range(3):
-            pltpu.make_async_copy(pack[a], send[a].at[c], pack_sem.at[a]).wait()
-
+        pieces, scale = [], jnp.zeros((16, LINE, 1), F32)
+        for m in range(4):
+            table = jnp.broadcast_to(tab_s[a, m, these, :][:, None, :], shape)
+            weight = jnp.broadcast_to(wt_s[a, m, these, :][:, None, :], shape)
+            pick = jnp.where((member == m) & (table == slot), 1.0, 0.0)
+            scale = scale + jnp.sum(pick * weight, axis=2, keepdims=True)
+            pieces.append(pick.reshape(ROWS, tokens).astype(BF))
+        return jnp.concatenate(pieces, axis=1), scale.reshape(ROWS, 1)
+
+    def packed(a, c, kind):
+        return pltpu.make_async_copy(pack[a].at[kind], send[a].at[c, kind], pack_sem.at[2 * a + kind])
+
+    def packing(c, kinds):
+        for a in range(3):
+            left, scale = picked(a, c)
+            for kind in kinds:
+                rows = dot(left, (line_rows, line_cots)[kind][a][...].reshape(4 * tokens, PART[a][1]))
+                pack[a][kind] = (rows if kind == 0 else rows * scale).astype(BF)
+                packed(a, c, kind).start()
+        for a in range(3):
+            for kind in kinds:
+                packed(a, c, kind).wait()
+
+    def issue(c):
         @pl.loop(0, 15)
         def _(i):
             for a in range(3):
-                forth(a, c, scattered(i)).start()
+                forth(a, c, scattered(i), BOTH).start()
 
         @pl.when(c % 2 == 1)
         def _():
             for a in range(3):
-                forth(a, c, 0).start()
+                forth(a, c, 0, BOTH).start()
 
         @pl.when(c % 2 == 0)
         def _():
             for a in range(3):
                 pltpu.make_async_copy(send[a].at[c, :, at(0)], came[a].at[c, :, at(0)], f_recv.at[c * 3 + a]).start()
+
+    for kind in range(2):
+        for a in range(3):
+            landed(a, 1 + kind, (line_rows, line_cots)[kind][a].at[three])
+        packing(0, (kind,))
+
+        @pl.loop(0, 15)
+        def _(i):
+            for a in range(3):
+                forth(a, 0, scattered(i), pl.ds(kind, 1)).start()
+
+        for a in range(3):
+            own = (0, kind, at(0))
+            pltpu.make_async_copy(send[a].at[own], came[a].at[own], f_recv.at[a]).start()
+
+    @pl.loop(1, CHUNKS)
+    def _(c):
+        packing(c, (0, 1))
+        issue(c)
 
     for c in loads:
         c.wait()
@@ -263,28 +296,27 @@
     spread_at = lax.broadcasted_iota(jnp.int32, (16, ROWS), 1) - LINE * lax.broadcasted_iota(jnp.int32, (16, ROWS), 0)
     spread = jnp.where((spread_at >= 0) & (spread_at < LINE), 1.0, 0.0).astype(BF)
 
-    @pl.loop(0, CHUNKS)
+    def gathered(c, a):
+        pltpu.make_async_copy(back[a].at[c], back[a].at[c], r_recv.at[c * 3 + a]).wait()
+        load = pltpu.make_async_copy(back[a].at[c], into[a].at[0], load_sem.at[a])
+        load.start()
+        pieces = []
+        for m in range(4):
+            table = dot(tab_s[a, m, pl.ds(pl.multiple_of(c * 16, 16), 16), :].astype(BF), spread, 0, 0)
+            pieces.append(jnp.where((part_ref[...] == float(m)) & (table == slot_ref[...]), 1.0, 0.0).astype(BF))
+        left = jnp.concatenate(pieces, axis=0)
+        load.wait()
+        sums[a][...] += dot(left, into[a][0])
+
+    @pl.loop(0, CHUNKS - 1)
     def _(c):
-        these = pl.ds(pl.multiple_of(c * 16, 16), 16)
-        for a in range(3):
-            pltpu.make_async_copy(back[a].at[c], back[a].at[c], r_recv.at[c * 3 + a]).wait()
-        for a in range(3):
-            pltpu.make_async_copy(back[a].at[c], into[a].at[0], load_sem.at[a]).start()
-        for a in range(3):
-            pieces = []
-            for m in range(4):
-                table = dot(tab_s[a, m, these, :].astype(BF), spread, 0, 0)
-                pieces.append(
-                    jnp.where((part_ref[...] == float(m)) & (table == slot_ref[...]), 1.0, 0.0).astype(BF)
-                )
-            left = jnp.concatenate(pieces, axis=0)
-            pltpu.make_async_copy(back[a].at[c], into[a].at[0], load_sem.at[a]).wait()
-            sums[a][...] += dot(left, into[a][0])
-
-    for a in range(3):
+        for a in range(3):
+            gathered(c, a)
+
+    for a in range(3):
+        gathered(CHUNKS - 1, a)
         line_rows[a][...] = sums[a][...].reshape(4, tokens, PART[a][1]).astype(BF)
-    for m in (2, 1, 3):
-        for a in range(3):
+        for m in (2, 1, 3):
             pltpu.make_async_remote_copy(
                 line_rows[a].at[m], near[a].at[m], l_send.at[a], l_recv.at[a],
                 device_id=device_at(along(a, -m), 0), device_id_type=MESH,
@@ -308,19 +340,11 @@
 
     for a in range(3):
         pltpu.make_async_copy(near[a].at[three], near[a].at[three], l_recv.at[a]).wait()
-    summed = jnp.concatenate(
-        [
+    for a in range(3):
+        lanes = slice(PART[a][0], PART[a][0] + PART[a][1])
+        summed_ref[:, lanes] = (
             sums[a][0:tokens, :] + near[a][1].astype(F32) + near[a][2].astype(F32) + near[a][3].astype(F32)
-            for a in range(3)
-        ],
-        axis=1,
-    )
-    raw = hid_ref[...].astype(F32)
-    root = lax.rsqrt(jnp.mean(raw * raw, axis=1, keepdims=True) + EPSILON)
-    scaled = raw * root
-    gained = summed * gain_ref[...]
-    centre = jnp.mean(gained * scaled, axis=1, keepdims=True)
-    hidden_ref[...] = (cot_ref[...].astype(F32) + root * (gained - scaled * centre)).astype(BF)
+        )
 
     seven = share_in_s.at[pl.ds(1, 7)]
     pltpu.make_async_copy(seven, seven, t_recv.at[1]).wait()
@@ -362,12 +386,12 @@
     both = [pltpu.VMEM((2, ROWS, size), BF) for size in sizes]
     outs = pl.pallas_call(
         core_kernel,
-        out_shape=[shape((tokens, width), BF), shape((1, 128), F32)]
+        out_shape=[shape((tokens, width), F32), shape((1, width), F32), shape((1, 128), F32)]
         + pairs * 2
         + singles * 2
         + [shape(gate.shape, BF), shape(up.shape, BF), shape(down.shape, BF)],
         in_specs=[vmem] * 4 + [hbm] * 4 + [vmem] * 3,
-        out_specs=[vmem] * 2 + [hbm] * 15,
+        out_specs=[vmem] * 3 + [hbm] * 15,
         scratch_shapes=[
             pltpu.VMEM((3, 4, 24, tokens), F32),
             pltpu.VMEM((3, 4, CHUNKS * 16, tokens), F32),
@@ -378,7 +402,6 @@
         + [pltpu.VMEM((4 * tokens, size), F32) for size in sizes]
         + line
         + [
-            pltpu.VMEM((1, width), F32),
             pltpu.VMEM((16, 1, 128), F32),
             pltpu.VMEM(gate.shape, BF),
             pltpu.VMEM(up.shape, BF),
@@ -394,7 +417,7 @@
             pltpu.VMEM((16, 1, 128), F32),
             pltpu.VMEM((1, 128), F32),
             pltpu.VMEM((8, 1, 128), F32),
-            dma((9,)), dma((9,)), dma((3,)), dma((3,)), dma, dma, dma((12,)), dma((12,)), dma((12,)), dma((12,)),
+            dma((9,)), dma((9,)), dma((6,)), dma((3,)), dma, dma, dma((12,)), dma((12,)), dma((12,)), dma((12,)),
             dma((3,)), dma((6,)), dma((2,)), dma((2,)), dma((3,)), dma((3,)),
         ],
         compiler_params=pltpu.CompilerParams(has_side_effects=True, vmem_limit_bytes=VMEM_LIMIT),
@@ -404,7 +427,53 @@
         meta, dest, hidden, cot, gain, gate, up, down,
         jnp.asarray(np.stack([order(a) for a in range(3)]), BF), slot, part,
     )
-    return outs[0], outs[1], outs[-3], outs[-2], outs[-1]
+    return outs[:3], outs[-3:]
+
+
+def finish_kernel(
+    summed_ref, gain_ref, total_ref, hid_ref, cot_ref, gate, up, down,
+    hidden_ref, share_ref, d_gate, d_up, d_down, gate_s, up_s, down_s, in_sem, out_sem,
+):
+    moves = [(gate, gate_s, d_gate), (up, up_s, d_up), (down, down_s, d_down)]
+    pieces = [
+        (
+            pltpu.make_async_copy(src.at[w], mid.at[w], in_sem.at[w, n]),
+            pltpu.make_async_copy(mid.at[w], out.at[w], out_sem.at[w, n]),
+        )
+        for w in range(2)
+        for n, (src, mid, out) in enumerate(moves)
+    ]
+    for into, _ in pieces:
+        into.start()
+    raw = hid_ref[...].astype(F32)
+    root = lax.rsqrt(jnp.mean(raw * raw, axis=1, keepdims=True) + EPSILON)
+    scaled = raw * root
+    gained = summed_ref[...] * gain_ref[...]
+    centre = jnp.mean(gained * scaled, axis=1, keepdims=True)
+    for into, out in pieces:
+        into.wait()
+        out.start()
+    hidden_ref[...] = (cot_ref[...].astype(F32) + root * (gained - scaled * centre)).astype(BF)
+    share_ref[...] = total_ref[...]
+    for _, out in pieces:
+        out.wait()
+
+
+def finish(sums, hidden, cot, grads):
+    hbm = pl.BlockSpec(memory_space=pl.ANY)
+    vmem = pl.BlockSpec(memory_space=pltpu.VMEM)
+    shape = lambda x: jax.ShapeDtypeStruct(x.shape, x.dtype)
+    return pl.pallas_call(
+        finish_kernel,
+        out_shape=[shape(hidden), shape(sums[2])] + [shape(g) for g in grads],
+        in_specs=[vmem] * 5 + [hbm] * 3,
+        out_specs=[vmem] * 2 + [hbm] * 3,
+        scratch_shapes=[pltpu.VMEM(g.shape, BF) for g in grads]
+        + [pltpu.SemaphoreType.DMA((2, 3)), pltpu.SemaphoreType.DMA((2, 3))],
+        compiler_params=pltpu.CompilerParams(vmem_limit_bytes=VMEM_LIMIT),
+        cost_estimate=pl.CostEstimate(flops=10**7, bytes_accessed=27 * 10**6, transcendentals=0),
+        name="finish",
+    )(*sums, hidden, cot, *grads)
 
 
 def shards(
@@ -418,9 +487,9 @@
         dp, seq = device_at(across(a, n % 16, 1), (n // 16) % 2)
         dest.append(2 * (dp * 8 + seq) + n // 32)
     dest = jnp.stack(dest).astype(F32)[:, :, None]
-    grad_hidden, grad_gain, grad_gate, grad_up, grad_down = core(
-        meta, dest, hidden_in[0], cotangent[0], norm_gain.reshape(1, -1), expert_gate, expert_up, expert_down
-    )
+    hidden, cot = hidden_in[0], cotangent[0]
+    sums, grads = core(meta, dest, hidden, cot, norm_gain.reshape(1, -1), expert_gate, expert_up, expert_down)
+    grad_hidden, grad_gain, grad_gate, grad_up, grad_down = finish(sums, hidden, cot, grads)
     return grad_hidden[None], grad_gain.reshape(-1), grad_gate, grad_up, grad_down
 
 

time: 219 us -> 208 us (0.950)
  local copies, waits for them, and re-layouts: 14.9 us -> 1.45 us
    unnamed x10 -> x1, local copies, waits for them, and re-layouts: 14.1 us -> 0.69 us
    pallas_call x1 -> x2, Pallas kernels: 200 us -> 202 us  [the longest x1 190 us: core(): pl.pallas_call(core_kernel, out_shape=[shape((tokens, width), F32), shape...]
where the time goes in v6:
time: 208 us; the launch traced here: 205 us
  Pallas kernels  202 us (97%)
    pallas_call x1, Pallas kernels, core(): pl.pallas_call(core_kernel, out_shape=[shape((tokens, width), F32), shape...  190 us
    pallas_call x1, Pallas kernels, finish(): pl.pallas_call(finish_kernel, out_shape=[shape(hidden), shape(sums[2])] +...  11.4 us

profile of v6, /device:TPU:1, one launch (start us, length us, event | category | flops | bytes accessed | tf_op | source)
XLA Modules:
  0.0 205.5 jit_solution(9600894439884340224)
XLA Ops:
  0.8 0.7 copy.29
  1.5 0.7 fusion
  2.2 0.6 pad_maximum_fusion.meta_ref
  2.8 0.8 copy.23.dest_ref
  3.5 190.4 %core.1 = (f32[128,2048]{1,0:T(8,128)}, f32[1,2048]{1,0:T(1,128)}, f32[1,128]{1,0:T(1,128)}, bf16[4,2,384,640]{3,2,1,0:T(8,128)(2,1)}, bf16[4,2,384,640]{3,2,1,0...) custom-call(f32[24,128]{1,0:T(8,128)} %pad_maximum_fusion.meta_ref, ...), custom_call_target="tpu_custom_call" | custom-call | flops 60000002048 | bytes 80000000 | tf_op jit(solution)/shard_map/core/pallas_call | solution.py:387
  193.9 11.4 %finish.1 = (bf16[128,2048]{1,0:T(8,128)(2,1)}, f32[1,128]{1,0:T(1,128)}, bf16[2,2048,512]{2,1,0:T(8,128)(2,1)}, bf16[2,2048,512]{2,1,0:T(8,128)(2,1)}, bf16[2,512,2048]{2,1,0:T(8,128)(2,1)}) custom-call(f32[128,2048]{1,0:T(8,128)} %get-tuple-element.16.summed_ref, f32[1,2048]{1,0:T(1,128)} %get-tuple-element.17.gain_ref, ...), custom_call_target="tpu_custom_call" | custom-call | flops 10000000 | bytes 27000000 | tf_op jit(solution)/shard_map/finish/pallas_call | solution.py:466
  (4 shorter events, 0.1 us)
